TPU v7x, 512 devices: a whole 4x8x8 slice. The times are simulated.
512 devices in a mesh: gx: 32 (over z, x), gy: 16 (over y, core).
Axes of the slice: x: 4, y: 8, z: 8, core: 2. Of those that a mesh axis runs over, the one named last changes fastest.
Arguments:
- basis: float32 [64, 2048, 2048], P(None, 'gx', 'gy'), may hold values from -6 to 6
- panel: float32 [8, 2048, 2048], P(None, 'gx', 'gy'), may hold values from -12 to 12
- rate_codes: int32 [4, 2048, 2048], P(None, 'gx', 'gy'), may hold values from 1 to 16
Outputs:
- first_panel: float32 [8, 2048, 2048], P(None, 'gx', 'gy')
- second_panel: float32 [8, 2048, 2048], P(None, 'gx', 'gy')
- first_coef: float32 [72, 8], replicated
- second_coef: float32 [80, 8], replicated
All inputs are finite; a program needn't handle non-finite values.
Results may differ from a plain program's by a relative error of at most 0.00014.
Values sent between devices are 32-bit elements; how exact they have to be, the bound alone decides.
A program may use at most 64 MiB of HBM per device.

v0:
```python
import jax
import jax.numpy as jnp
from jax import lax
from jax.sharding import Mesh
from jax.sharding import PartitionSpec as P

GX = ("gx_0", "gx_1")
GY = ("gy_0", "gy_1")


HIGH = lax.Precision.HIGHEST


def from_everyone(array, axis):
    count = lax.axis_size(axis)
    return lax.all_to_all(
        jnp.broadcast_to(array[None], (count, *array.shape)), axis, 0, 0, tiled=True
    )


def of_everyone(array, axis):
    return from_everyone(array, axis).sum(axis=0)


def by_axis(array, axes):
    far, near = axes
    nearer = of_everyone(array, near)
    return of_everyone(nearer, far)


def in_one(arrays, axis):
    ends = [0]
    for a in arrays:
        ends.append(ends[-1] + a.size)
    total = by_axis(jnp.concatenate([a.ravel() for a in arrays]), axis)
    return tuple((total[b:e].reshape(a.shape) for a, b, e in zip(arrays, ends, ends[1:])))


def from_behind(block, axis, distance):
    devices = range(lax.axis_size(axis))
    route = [(i - distance, i) for i in devices if i - distance in devices]
    return lax.ppermute(block, axis, route)


def tri_inverse(lower_fac):
    width_cols = lower_fac.shape[0]
    return lax.linalg.triangular_solve(
        lower_fac, jnp.eye(width_cols, dtype=jnp.float32), left_side=True, lower=True
    )


def joint_reduce(first_term, second_term):
    return in_one((first_term, second_term), (("gx_0", "gx_1"), ("gy_0", "gy_1")))


def local(basis, panel, rate_codes):
    block_cols, lat_rows, lat_cols = panel.shape
    basis_cols = basis.shape[0]
    site_count = jnp.float32(lat_rows * lat_cols * lax.axis_size(GX) * lax.axis_size(GY))
    rate_vals = rate_codes.astype(jnp.float32) * 0.125
    total_rate = jnp.sum(rate_vals, axis=0)

    def lattice_apply(field):
        flow_up = rate_vals[0] * field
        flow_down = rate_vals[1] * field
        flow_left = rate_vals[2] * field
        flow_right = rate_vals[3] * field
        from_above = jnp.concatenate(
            [from_behind(flow_down[:, -1:, :], GX, 1), flow_down[:, :-1, :]], axis=1
        )
        from_below = jnp.concatenate(
            [flow_up[:, 1:, :], from_behind(flow_up[:, :1, :], GX, -1)], axis=1
        )
        from_leftside = jnp.concatenate(
            [from_behind(flow_right[:, :, -1:], GY, 1), flow_right[:, :, :-1]], axis=2
        )
        from_rightside = jnp.concatenate(
            [flow_left[:, :, 1:], from_behind(flow_left[:, :, :1], GY, -1)], axis=2
        )
        inflow = from_above + from_below + from_leftside + from_rightside
        return inflow - total_rate * field

    basis_flat = basis.reshape(basis_cols, lat_rows * lat_cols)
    image_one = lattice_apply(panel).reshape(block_cols, lat_rows * lat_cols)

    def finish(space, image, proj_coef, panel_gram, space_gram):
        gram_mat = (
            panel_gram
            - 2.0 * jnp.dot(proj_coef.T, proj_coef, precision=HIGH)
            + jnp.dot(proj_coef.T, jnp.dot(space_gram, proj_coef, precision=HIGH), precision=HIGH)
        )
        cleaned = image - jnp.dot(proj_coef.T, space, precision=HIGH)
        lower_fac = jnp.linalg.cholesky(gram_mat)
        inverse_fac = tri_inverse(lower_fac)
        new_panel = jnp.dot(inverse_fac, cleaned, precision=HIGH)
        return (new_panel, lower_fac, inverse_fac, gram_mat)

    stacked = jnp.concatenate([image_one, basis_flat], axis=0)
    cross_sum, wgram_sum = joint_reduce(
        jnp.dot(basis_flat, stacked.T, precision=HIGH),
        jnp.dot(image_one, image_one.T, precision=HIGH),
    )
    proj_one = cross_sum[:, :block_cols] / site_count
    space_gram = cross_sum[:, block_cols:] / site_count
    first_flat, lower_one, inverse_one, gram_one = finish(
        basis_flat, image_one, proj_one, wgram_sum / site_count, space_gram
    )
    first_coef = jnp.concatenate([proj_one, lower_one.T], axis=0)
    first_panel = first_flat.reshape(block_cols, lat_rows, lat_cols)
    image_two = lattice_apply(first_panel).reshape(block_cols, lat_rows * lat_cols)
    grown = jnp.concatenate([basis_flat, first_flat], axis=0)
    basis_new = jnp.dot(
        proj_one - jnp.dot(space_gram, proj_one, precision=HIGH), inverse_one.T, precision=HIGH
    )
    new_new = jnp.dot(inverse_one, jnp.dot(gram_one, inverse_one.T, precision=HIGH), precision=HIGH)
    grown_gram = jnp.concatenate(
        [
            jnp.concatenate([space_gram, basis_new], axis=1),
            jnp.concatenate([basis_new.T, new_new], axis=1),
        ],
        axis=0,
    )
    proj_sum, pgram_sum = joint_reduce(
        jnp.dot(grown, image_two.T, precision=HIGH), jnp.dot(image_two, image_two.T, precision=HIGH)
    )
    proj_two = proj_sum / site_count
    second_flat, lower_two, inverse_two, gram_two = finish(
        grown, image_two, proj_two, pgram_sum / site_count, grown_gram
    )
    second_coef = jnp.concatenate([proj_two, lower_two.T], axis=0)
    second_panel = second_flat.reshape(block_cols, lat_rows, lat_cols)
    return (first_panel, second_panel, first_coef, second_coef)


def solution(mesh):
    split = Mesh(mesh.devices.reshape(8, 4, 8, 2), ("gx_0", "gx_1", "gy_0", "gy_1"))
    placed = (P(None, GX, GY), P(None, GX, GY), P(None, GX, GY))
    return jax.shard_map(
        local,
        mesh=split,
        in_specs=placed,
        out_specs=(P(None, GX, GY), P(None, GX, GY), P(), P()),
        check_vma=False,
    )
```

profile of v0, /device:TPU:1, one launch (start us, length us, event | category | flops | bytes accessed | tf_op | source)
XLA Modules:
  0.0 141.7 jit_solution(12887111615407989319)
XLA Ops:
  0.6 1.1 fusion.46
  1.7 1.1 broadcast_multiply_fusion.1
  2.8 3.9 %collective-permute-start = (f32[8,1,128]{2,1,0:T(1,128)S(1)}, f32[8,1,128]{2,1,0:T(1,128)S(1)}, u32[]{:S(2)}, u32[]{:S(2)}) collective-permute-start(f32[8,1,128]{2,1,0:T(1,128)S(1)} %slice.143), channel_id=1, source_target_pairs={{0,16},{16,32},{32,48},{48,64},{64,80},{80,96},{96,112},{112,128},... | collective-permute-start | bytes 12296 | tf_op jit(solution)/shard_map/ppermute | solution.py:42
  6.8 1.3 collective-permute-start.1
  8.2 4.0 %collective-permute-start.2 = (f32[8,64,1]{2,1,0:T(8,128)S(1)}, f32[8,64,1]{2,1,0:T(8,128)S(1)}, u32[]{:S(2)}, u32[]{:S(2)}) collective-permute-start(f32[8,64,1]{2,1,0:T(8,128)S(1)} %slice.149), channel_id=1, source_target_pairs={{0,1},{1,2},{2,3},{3,4},{4,5},{5,6},{6,7},{7,8},{8,9},{9,10},{10,1... | collective-permute-start | bytes 6152 | tf_op jit(solution)/shard_map/ppermute | solution.py:42
  12.3 3.4 %collective-permute-start.3 = (f32[8,64,1]{2,1,0:T(8,128)S(1)}, f32[8,64,1]{2,1,0:T(8,128)S(1)}, u32[]{:S(2)}, u32[]{:S(2)}) collective-permute-start(f32[8,64,1]{2,1,0:T(8,128)S(1)} %bitcast.99), channel_id=1, source_target_pairs={{1,0},{2,1},{3,2},{4,3},{5,4},{6,5},{7,6},{8,7},{9,8},{10,9},{11,1... | collective-permute-start | bytes 6152 | tf_op jit(solution)/shard_map/ppermute | solution.py:42
  15.8 1.2 copy.149
  17.0 2.9 %collective-permute-done.3 = f32[8,64,1]{2,1,0:T(8,128)S(1)} collective-permute-done((f32[8,64,1]{2,1,0:T(8,128)S(1)}, f32[8,64,1]{2,1,0:T(8,128)S(1)}, u32[]{:S(2)}, u32[]{:S(2)}) %collective-permute-start.3) | collective-permute-done | bytes 2080 | tf_op jit(solution)/shard_map/ppermute | solution.py:42
  20.0 0.2 fusion.12
  20.2 0.7 convolution_bitcast_fusion.1
  21.2 2.0 %fusion.5 = f32[64,72]{1,0:T(8,128)S(1)} fusion(f32[64,8192]{1,0:T(8,128)S(1)} %bitcast.85, f32[8,8192]{1,0:T(8,128)S(1)} %bitcast.98), kind=kOutput, calls=%fused_computation.10 | convolution fusion | flops 453574656 | bytes 2377728 | tf_op jit(solution)/shard_map/dot_general | solution.py:100
  23.4 19.7 %all_to_all.24 = f32[16,1,4672]{2,1,0:T(1,128)S(1)} all-to-all(f32[16,1,4672]{2,1,0:T(1,128)S(1)} %broadcast_in_dim.8), channel_id=1, replica_groups=mesh['gx_0'=8,'gx_1'=4,'gy_0'=8,'gy_1'=2] {'gy_0','gy_1'}, dimensions={0} | all-to-all | bytes 598016 | tf_op jit(solution)/shard_map/all_to_all | solution.py:16
  43.3 0.3 broadcast_in_dim.9
  43.6 33.4 %all_to_all.25 = f32[32,1,4672]{2,1,0:T(1,128)S(1)} all-to-all(f32[32,1,4672]{2,1,0:T(1,128)S(1)} %broadcast_in_dim.9), channel_id=1, replica_groups=mesh['gx_0'=8,'gx_1'=4,'gy_0'=8,'gy_1'=2] {'gx_0','gx_1'}, dimensions={0} | all-to-all | bytes 1196032 | tf_op jit(solution)/shard_map/all_to_all | solution.py:16
  77.1 0.4 reduce_sum.47
  77.6 0.2 fusion.45
  77.8 3.8 %convolution_subtract_fusion.1 = f32[8,8192]{1,0:T(8,128)S(1)} fusion(f32[64,8]{0,1:T(8,128)S(1)} %copy.130, f32[1,8,64,128]{3,2,1,0:T(8,128)S(1)} %bitcast.92, f32[8,8,64,128]{3,2,1,0:T(8,128)} %bitcast.89), kind=kOutput, calls=%fused_computation.1 | convolution fusion | flops 50397696 | bytes 2623488 | tf_op jit(solution)/shard_map/dot_general | solution.py:92
  82.2 0.7 cholesky.44
  83.0 0.6 compare_reduce_fusion.1
  83.6 0.6 fusion.39
  84.3 0.6 custom-call.6
  85.2 0.4 fusion.47
  85.8 3.3 %collective-permute-start.4 = (f32[8,1,128]{2,1,0:T(1,128)S(1)}, f32[8,1,128]{2,1,0:T(1,128)S(1)}, u32[]{:S(2)}, u32[]{:S(2)}) collective-permute-start(f32[8,1,128]{2,1,0:T(1,128)S(1)} %slice.158), channel_id=1, source_target_pairs={{0,16},{16,32},{32,48},{48,64},{64,80},{80,96},{96,112},{112,128},... | collective-permute-start | bytes 12296 | tf_op jit(solution)/shard_map/ppermute | solution.py:42
  89.1 1.3 collective-permute-start.5
  90.5 2.5 %collective-permute-start.6 = (f32[8,64,1]{2,1,0:T(8,128)S(1)}, f32[8,64,1]{2,1,0:T(8,128)S(1)}, u32[]{:S(2)}, u32[]{:S(2)}) collective-permute-start(f32[8,64,1]{2,1,0:T(8,128)S(1)} %slice.162), channel_id=1, source_target_pairs={{0,1},{1,2},{2,3},{3,4},{4,5},{5,6},{6,7},{7,8},{8,9},{9,10},{10,1... | collective-permute-start | bytes 6152 | tf_op jit(solution)/shard_map/ppermute | solution.py:42
  93.0 2.1 %collective-permute-start.7 = (f32[8,64,1]{2,1,0:T(8,128)S(1)}, f32[8,64,1]{2,1,0:T(8,128)S(1)}, u32[]{:S(2)}, u32[]{:S(2)}) collective-permute-start(f32[8,64,1]{2,1,0:T(8,128)S(1)} %bitcast.97), channel_id=1, source_target_pairs={{1,0},{2,1},{3,2},{4,3},{5,4},{6,5},{7,6},{8,7},{9,8},{10,9},{11,1... | collective-permute-start | bytes 6152 | tf_op jit(solution)/shard_map/ppermute | solution.py:42
  95.5 0.8 collective-permute-done.6
  96.3 4.4 %collective-permute-done.7 = f32[8,64,1]{2,1,0:T(8,128)S(1)} collective-permute-done((f32[8,64,1]{2,1,0:T(8,128)S(1)}, f32[8,64,1]{2,1,0:T(8,128)S(1)}, u32[]{:S(2)}, u32[]{:S(2)}) %collective-permute-start.7) | collective-permute-done | bytes 2080 | tf_op jit(solution)/shard_map/ppermute | solution.py:42
  100.7 0.2 fusion.15
  100.9 0.7 fusion.17
  101.6 2.0 %fusion.4 = f32[72,8]{1,0:T(8,128)S(1)} fusion(f32[8,8192]{1,0:T(8,128)S(1)} %fusion.47, f32[64,8192]{1,0:T(8,128)S(1)} %bitcast.86, f32[1,8,64,128]{3,2,1,0:T(8,128)S(1)} %fusion.15, f32[8192]{0:T(1024)S(1)} %bitcast.101), kind=kOutput, calls=%fused_computation.8 | convolution fusion | flops 57344000 | bytes 2656512 | tf_op jit(solution)/shard_map/dot_general | solution.py:124
  103.9 0.6 broadcast_in_dim.11
  104.5 4.7 %all-to-all-start.2 = ((f32[16,1,640]{2,1,0:T(1,128)}), f32[16,1,640]{2,1,0:T(1,128)S(1)}, u32[]{:S(2)}, u32[]{:S(2)}) async-start(f32[16,1,640]{2,1,0:T(1,128)} %broadcast_in_dim.11), calls=%async_computation.2 | async-start | bytes 81920 | tf_op jit(solution)/shard_map/all_to_all | solution.py:16
  109.4 7.3 %all-to-all-done.2 = f32[16,1,640]{2,1,0:T(1,128)S(1)} async-done(((f32[16,1,640]{2,1,0:T(1,128)}), f32[16,1,640]{2,1,0:T(1,128)S(1)}, u32[]{:S(2)}, u32[]{:S(2)}) %all-to-all-start.2) | async-done | bytes 40992 | tf_op jit(solution)/shard_map/all_to_all | solution.py:16
  116.7 0.7 broadcast_in_dim.12
  117.4 8.2 %all-to-all-start.3 = ((f32[32,1,640]{2,1,0:T(1,128)}), f32[32,1,640]{2,1,0:T(1,128)S(1)}, u32[]{:S(2)}, u32[]{:S(2)}) async-start(f32[32,1,640]{2,1,0:T(1,128)} %broadcast_in_dim.12), calls=%async_computation.3 | async-start | bytes 163840 | tf_op jit(solution)/shard_map/all_to_all | solution.py:16
  125.7 0.7 pad_maximum_fusion.5
  126.4 8.2 %all-to-all-done.3 = f32[32,1,640]{2,1,0:T(1,128)S(1)} async-done(((f32[32,1,640]{2,1,0:T(1,128)}), f32[32,1,640]{2,1,0:T(1,128)S(1)}, u32[]{:S(2)}, u32[]{:S(2)}) %all-to-all-start.3) | async-done | bytes 81952 | tf_op jit(solution)/shard_map/all_to_all | solution.py:16
  134.8 1.3 convolution_subtract_fusion
  136.3 0.2 fusion.8
  136.5 0.3 fusion.20
  137.0 0.7 cholesky.55
  137.8 0.6 compare_reduce_fusion
  138.4 0.6 fusion.40
  139.1 0.6 custom-call.7
  139.9 0.4 convolution_bitcast_fusion
  140.3 0.8 copy.118
  141.0 0.7 pad_maximum_fusion.6
  (63 shorter events, 4.2 us)
Async XLA Ops:
  0.6 15.2 %copy-start = (f32[64,64,128]{2,1,0:T(8,128)S(1)}, f32[64,64,128]{2,1,0:T(8,128)}, u32[]{:S(2)}) copy-start(f32[64,64,128]{2,1,0:T(8,128)} %param.6) | copy-start | bytes 6291460
  2.8 17.1 %collective-permute-start = (f32[8,1,128]{2,1,0:T(1,128)S(1)}, f32[8,1,128]{2,1,0:T(1,128)S(1)}, u32[]{:S(2)}, u32[]{:S(2)}) collective-permute-start(f32[8,1,128]{2,1,0:T(1,128)S(1)} %slice.143), channel_id=1, source_target_pairs={{0,16},{16,32},{32,48},{48,64},{64,80},{80,96},{96,112},{112,128},... | collective-permute-start | bytes 12296 | tf_op jit(solution)/shard_map/ppermute | solution.py:42
  6.8 13.2 %collective-permute-start.1 = (f32[8,1,128]{2,1,0:T(1,128)S(1)}, f32[8,1,128]{2,1,0:T(1,128)S(1)}, u32[]{:S(2)}, u32[]{:S(2)}) collective-permute-start(f32[8,1,128]{2,1,0:T(1,128)S(1)} %slice.147), channel_id=1, source_target_pairs={{16,0},{32,16},{48,32},{64,48},{80,64},{96,80},{112,96},{128,112},... | collective-permute-start | bytes 12296 | tf_op jit(solution)/shard_map/ppermute | solution.py:42
  8.2 8.8 %collective-permute-start.2 = (f32[8,64,1]{2,1,0:T(8,128)S(1)}, f32[8,64,1]{2,1,0:T(8,128)S(1)}, u32[]{:S(2)}, u32[]{:S(2)}) collective-permute-start(f32[8,64,1]{2,1,0:T(8,128)S(1)} %slice.149), channel_id=1, source_target_pairs={{0,1},{1,2},{2,3},{3,4},{4,5},{5,6},{6,7},{7,8},{8,9},{9,10},{10,1... | collective-permute-start | bytes 6152 | tf_op jit(solution)/shard_map/ppermute | solution.py:42
  12.3 7.7 %collective-permute-start.3 = (f32[8,64,1]{2,1,0:T(8,128)S(1)}, f32[8,64,1]{2,1,0:T(8,128)S(1)}, u32[]{:S(2)}, u32[]{:S(2)}) collective-permute-start(f32[8,64,1]{2,1,0:T(8,128)S(1)} %bitcast.99), channel_id=1, source_target_pairs={{1,0},{2,1},{3,2},{4,3},{5,4},{6,5},{7,6},{8,7},{9,8},{10,9},{11,1... | collective-permute-start | bytes 6152 | tf_op jit(solution)/shard_map/ppermute | solution.py:42
  15.8 4.2 %copy-start.2 = (f32[8,64,128]{2,1,0:T(8,128)S(1)}, f32[8,64,128]{2,1,0:T(8,128)}, u32[]{:S(2)}) copy-start(f32[8,64,128]{2,1,0:T(8,128)} %param.7) | copy-start | bytes 786436
  85.7 15.3 %copy-start.1 = (f32[8,64,128]{2,1,0:T(8,128)}, f32[8,64,128]{2,1,0:T(8,128)S(1)}, u32[]{:S(2)}) copy-start(f32[8,64,128]{2,1,0:T(8,128)S(1)} %get-tuple-element.27) | copy-start | bytes 786436
  85.8 14.9 %collective-permute-start.4 = (f32[8,1,128]{2,1,0:T(1,128)S(1)}, f32[8,1,128]{2,1,0:T(1,128)S(1)}, u32[]{:S(2)}, u32[]{:S(2)}) collective-permute-start(f32[8,1,128]{2,1,0:T(1,128)S(1)} %slice.158), channel_id=1, source_target_pairs={{0,16},{16,32},{32,48},{48,64},{64,80},{80,96},{96,112},{112,128},... | collective-permute-start | bytes 12296 | tf_op jit(solution)/shard_map/ppermute | solution.py:42
  89.1 11.6 %collective-permute-start.5 = (f32[8,1,128]{2,1,0:T(1,128)S(1)}, f32[8,1,128]{2,1,0:T(1,128)S(1)}, u32[]{:S(2)}, u32[]{:S(2)}) collective-permute-start(f32[8,1,128]{2,1,0:T(1,128)S(1)} %slice.161), channel_id=1, source_target_pairs={{16,0},{32,16},{48,32},{64,48},{80,64},{96,80},{112,96},{128,112},... | collective-permute-start | bytes 12296 | tf_op jit(solution)/shard_map/ppermute | solution.py:42
  90.5 5.8 %collective-permute-start.6 = (f32[8,64,1]{2,1,0:T(8,128)S(1)}, f32[8,64,1]{2,1,0:T(8,128)S(1)}, u32[]{:S(2)}, u32[]{:S(2)}) collective-permute-start(f32[8,64,1]{2,1,0:T(8,128)S(1)} %slice.162), channel_id=1, source_target_pairs={{0,1},{1,2},{2,3},{3,4},{4,5},{5,6},{6,7},{7,8},{8,9},{9,10},{10,1... | collective-permute-start | bytes 6152 | tf_op jit(solution)/shard_map/ppermute | solution.py:42
  93.0 7.7 %collective-permute-start.7 = (f32[8,64,1]{2,1,0:T(8,128)S(1)}, f32[8,64,1]{2,1,0:T(8,128)S(1)}, u32[]{:S(2)}, u32[]{:S(2)}) collective-permute-start(f32[8,64,1]{2,1,0:T(8,128)S(1)} %bitcast.97), channel_id=1, source_target_pairs={{1,0},{2,1},{3,2},{4,3},{5,4},{6,5},{7,6},{8,7},{9,8},{10,9},{11,1... | collective-permute-start | bytes 6152 | tf_op jit(solution)/shard_map/ppermute | solution.py:42
  104.5 12.1 %all-to-all-start.2 = ((f32[16,1,640]{2,1,0:T(1,128)}), f32[16,1,640]{2,1,0:T(1,128)S(1)}, u32[]{:S(2)}, u32[]{:S(2)}) async-start(f32[16,1,640]{2,1,0:T(1,128)} %broadcast_in_dim.11), calls=%async_computation.2 | async-start | bytes 81920 | tf_op jit(solution)/shard_map/all_to_all | solution.py:16
  117.4 17.2 %all-to-all-start.3 = ((f32[32,1,640]{2,1,0:T(1,128)}), f32[32,1,640]{2,1,0:T(1,128)S(1)}, u32[]{:S(2)}, u32[]{:S(2)}) async-start(f32[32,1,640]{2,1,0:T(1,128)} %broadcast_in_dim.12), calls=%async_computation.3 | async-start | bytes 163840 | tf_op jit(solution)/shard_map/all_to_all | solution.py:16
where the time goes:
time: 142 us
  blocking collectives  53.1 us (37%)
  starting transfers between devices  34.7 us (24%)
  waiting for transfers between devices  23.6 us (17%)
  matrix products  13.2 us (9%)
  other arithmetic  10.3 us (7%)
  local copies, waits for them, and re-layouts  5.66 us (4%)
    all_to_all x2, blocking collectives, from_everyone(): lax.all_to_all(jnp.broadcast_to(array[None], (count, *array.shape)), axis...  53.1 us
    ppermute x8, starting transfers between devices, from_behind(): return lax.ppermute(block, axis, route)  21.8 us
    all_to_all x2, waiting for transfers between devices, from_everyone(): lax.all_to_all(jnp.broadcast_to(array[None], (count, *array.shape)), axis...  15.5 us
    all_to_all x2, starting transfers between devices, from_everyone(): lax.all_to_all(jnp.broadcast_to(array[None], (count, *array.shape)), axis...  12.9 us
    ppermute x8, waiting for transfers between devices, from_behind(): return lax.ppermute(block, axis, route)  8.16 us
    dot_general x2, matrix products, finish(): cleaned = image - jnp.dot(proj_coef.T, space, precision=HIGH)  5.06 us
  transfers between devices with their start and end apart: 10, of which 5 were waited for; matrix products, arithmetic and copies ran while one was open for 2% of the time, Pallas kernels for 0%

commit v1 on v0

v1 whole, which is shorter than its diff:
```python
import functools

import jax
import jax.numpy as jnp
from jax import lax
from jax.experimental import pallas as pl
from jax.experimental.pallas import tpu as pltpu
from jax.sharding import PartitionSpec as P

HIGH = lax.Precision.HIGHEST
MESH = pl.DeviceIdType.MESH
F32 = jnp.float32
BF16 = jnp.bfloat16
NN = (((1,), (0,)), ((), ()))
NT = (((1,), (1,)), ((), ()))
LANES = 128


def small_dot(a, b, dims):
    return lax.dot_general(a, b, dims, precision=HIGH, preferred_element_type=F32)


def split_two(x):
    hi = x.astype(BF16)
    lo = (x - hi.astype(F32)).astype(BF16)
    return hi, lo


def eliminate(gram):
    n = gram.shape[0]
    row = lax.broadcasted_iota(jnp.int32, (n, n), 0)
    col = lax.broadcasted_iota(jnp.int32, (n, n), 1)
    left = gram
    right = jnp.where(row == col, 1.0, 0.0).astype(F32)
    for j in range(n):
        factor = jnp.where(row[:, :1] > j, left[:, j : j + 1] / left[j : j + 1, j : j + 1], 0.0)
        left, right = (left - factor * left[j : j + 1, :], right - factor * right[j : j + 1, :])
    diag = jnp.sum(jnp.where(row == col, left, 0.0), axis=1, keepdims=True)
    root = 1.0 / jnp.sqrt(diag)
    return jnp.where(row <= col, left * root, 0.0), right * root


def kernel(
    dims,
    xb_ref, xp_ref, codes_ref,
    q1_ref, q2_ref, co_ref, lt_ref,
    rf, up_x, dn_x, up_r, dn_r, pack_l, pack_r, from_l, from_r,
    w1, up_w, dn_w, wpack_l, wpack_r, wfrom_l, wfrom_r,
    z2, acc, payload, rs_buf, y_buf, z_buf, full,
    halo_send, halo_recv, red_send, red_recv,
):
    nz, nx, ny, rows, nb, np_, scale = dims
    nm = nx * 2
    chunk = payload.shape[0] // nm
    gx, gy = lax.axis_index("gx"), lax.axis_index("gy")
    zz, xx = gx // nx, gx % nx
    yy, core = gy // 2, gy % 2
    member = xx * 2 + core
    ngx, ngy = nz * nx, ny * 2
    above = ((gx + ngx - 1) % ngx, gy)
    below = ((gx + 1) % ngx, gy)
    left = (gx, (gy + ngy - 1) % ngy)
    right = (gx, (gy + 1) % ngy)

    def in_team(d):
        m = (member + d) % nm
        return (zz * nx + m // 2, yy * 2 + m % 2)

    def in_y(d):
        return (gx, ((yy + d) % ny) * 2 + core)

    def in_z(d):
        return (((zz + d) % nz) * nx + xx, gy)

    peers = [above, below, left, right]
    peers += [in_team(d) for d in range(1, nm)]
    peers += [in_y(d) for d in range(1, ny)]
    peers += [in_z(d) for d in range(1, nz)]
    barrier = pltpu.get_barrier_semaphore()
    for peer in peers:
        pl.semaphore_signal(barrier, inc=1, device_id=peer, device_id_type=MESH)

    nc = nb + np_
    nt = nb * 2 + np_ * 2
    lane = lax.broadcasted_iota(jnp.int32, (1, LANES), 1)

    codes = codes_ref[...].astype(F32) * 0.125
    rf[0:4] = codes
    rf[4] = codes[0] + codes[1] + codes[2] + codes[3]

    def rate(d, r):
        return rf[d, pl.ds(r, 1), :]

    def cols(ref, r):
        return ref[:, pl.ds(pl.multiple_of(r * LANES, LANES), LANES)]

    def pack_step(x, r, accs):
        y = jnp.where(lane == LANES - 1, rate(3, r) * x, rate(2, r) * x)
        y = pltpu.roll(y, r, 1)
        a, b = accs
        return (jnp.where(lane == r, y, a), jnp.where(lane == (r + LANES - 1) % LANES, y, b))

    def pack_b(r, accs):
        return pack_step(cols(xb_ref, r), r, accs)

    def pack_p(r, accs):
        return pack_step(cols(xp_ref, r), r, accs)

    zp = jnp.zeros((np_, LANES), F32)
    zb = jnp.zeros((nb, LANES), F32)
    a, b = lax.fori_loop(0, rows, pack_p, (zp, zp))
    pack_l[nb:nc] = a
    pack_r[nb:nc] = b
    a, b = lax.fori_loop(0, rows, pack_b, (zb, zb))
    pack_l[0:nb] = a
    pack_r[0:nb] = b

    pl.semaphore_wait(barrier, len(peers))

    last = (rows - 1) * LANES
    end = rows * LANES

    def halo(k, src, dst, peer):
        c = pltpu.make_async_remote_copy(
            src_ref=src, dst_ref=dst, send_sem=halo_send.at[k], recv_sem=halo_recv.at[k],
            device_id=peer, device_id_type=MESH,
        )
        c.start()
        return c

    small = [
        halo(0, xp_ref.at[:, last:end], up_x.at[nb:nc], below),
        halo(1, xp_ref.at[:, 0:LANES], dn_x.at[nb:nc], above),
        halo(2, pack_r.at[nb:nc], from_l.at[nb:nc], right),
        halo(3, pack_l.at[nb:nc], from_r.at[nb:nc], left),
        halo(4, codes_ref.at[1, rows - 8 : rows], up_r, below),
        halo(5, codes_ref.at[0, 0:8], dn_r, above),
    ]
    big = [
        halo(6, xb_ref.at[:, last:end], up_x.at[0:nb], below),
        halo(7, xb_ref.at[:, 0:LANES], dn_x.at[0:nb], above),
        halo(8, pack_r.at[0:nb], from_l.at[0:nb], right),
        halo(9, pack_l.at[0:nb], from_r.at[0:nb], left),
    ]

    def put(first, r, x):
        hi, lo = split_two(x)
        at = pl.ds(pl.multiple_of(r * LANES, LANES), LANES)
        z2[first : first + x.shape[0], at] = hi
        z2[nt + first : nt + first + x.shape[0], at] = lo

    def split_b(r, _):
        put(0, r, cols(xb_ref, r))
        return 0

    lax.fori_loop(0, rows, split_b, 0)

    def stencil(r, rate_u, rate_d, xu, x, xd, fl, fr):
        from_l = jnp.where(lane == 0, pltpu.roll(fl, (2 * LANES + 1 - r) % LANES, 1), pltpu.roll(rate(3, r) * x, 1, 1))
        from_r = jnp.where(
            lane == LANES - 1, pltpu.roll(fr, (2 * LANES - 1 - r) % LANES, 1), pltpu.roll(rate(2, r) * x, LANES - 1, 1)
        )
        return (rate_u * xu + rate_d * xd) + (from_l + from_r) - rate(4, r) * x

    def sweep(x_at, up, dn, fl, fr, emit, carry, unroll):
        e = rows - 1

        def group(rs, c):
            outs = []
            for r in rs:
                at_top, at_end = isinstance(r, int) and r == 0, isinstance(r, int) and r == e
                outs.append(
                    stencil(
                        r,
                        rate_up() if at_top else rate(1, r - 1),
                        rate_dn() if at_end else rate(0, r + 1),
                        up if at_top else x_at(r - 1),
                        x_at(r),
                        dn if at_end else x_at(r + 1),
                        fl, fr,
                    )
                )
            for r, out in zip(rs, outs):
                c = emit(r, out, c)
            return c

        trips = (rows - 2) // unroll
        carry = lax.fori_loop(
            0, trips, lambda k, c: group([1 + k * unroll + i for i in range(unroll)], c), carry
        )
        return group([0] + list(range(1 + trips * unroll, rows)), carry)

    def rate_up():
        return up_r[7:8, :].astype(F32) * 0.125

    def rate_dn():
        return dn_r[0:1, :].astype(F32) * 0.125

    keep = (gx > 0, gx < ngx - 1, gy > 0, gy < ngy - 1)

    def edged(values):
        return [v * jnp.where(k, 1.0, 0.0).astype(F32) for v, k in zip(values, keep)]

    for c in small:
        c.wait()

    def emit_w(r, out, accs):
        w1[:, pl.ds(pl.multiple_of(r * LANES, LANES), LANES)] = out
        return pack_step(out, r, accs)

    halos = edged([up_x[nb:nc], dn_x[nb:nc], from_l[nb:nc], from_r[nb:nc]])
    a, b = sweep(lambda r: cols(xp_ref, r), *halos, emit_w, (zp, zp), 12)
    wpack_l[...] = a
    wpack_r[...] = b
    wsend = [
        halo(10, w1.at[:, last:end], up_w, below),
        halo(11, w1.at[:, 0:LANES], dn_w, above),
        halo(12, wpack_r, wfrom_l, right),
        halo(13, wpack_l, wfrom_r, left),
    ]

    for c in big:
        c.wait()

    def emit_b(r, out, c):
        put(nb, r, out)
        return c

    halos = edged([up_x[0:nb], dn_x[0:nb], from_l[0:nb], from_r[0:nb]])
    sweep(lambda r: cols(xb_ref, r), *halos, emit_b, 0, 2)

    for c in wsend:
        c.wait()

    def emit_aw(r, out, c):
        put(2 * nb, r, jnp.concatenate([cols(w1, r), out], axis=0))
        return c

    halos = edged([up_w[...], dn_w[...], wfrom_l[...], wfrom_r[...]])
    sweep(lambda r: cols(w1, r), *halos, emit_aw, 0, 12)

    step = min(1024, end)
    acc[...] = jnp.zeros_like(acc)

    def gram_step(k, _):
        at = pl.ds(pl.multiple_of(k * step, step), step)
        acc[...] += lax.dot_general(z2[:, at], z2[0:nt, at], NT, preferred_element_type=F32)
        return 0

    lax.fori_loop(0, end // step, gram_step, 0)
    half = acc[0:nt, :] * 0.5 + acc[nt : 2 * nt, :]
    na = 2 * nb
    aa = half[0:na, 0:na]
    aa = aa + aa.T
    aw = jnp.concatenate([half[0:na, na:nt], jnp.zeros((na, LANES - (nt - na)), F32)], axis=1)
    wa = half[na:nt, 0:na] + aw.T[0 : nt - na, :]
    ww = half[na:nt, na:nt]
    ww = ww + ww.T
    lane_low = lane < nb
    payload[0:nb] = aa[0:nb]
    hb = nb // 2
    payload[nb : nb + hb] = jnp.where(lane_low, pltpu.roll(aa[nb : nb + hb], nb, 1), aa[nb + hb : na])
    base = nb + hb
    payload[base : base + 2 * np_] = wa
    payload[base + 2 * np_ : base + 4 * np_] = jnp.concatenate(
        [ww, jnp.zeros((2 * np_, LANES - 2 * np_), F32)], axis=1
    )

    def reduce_copy(k, src, dst, peer):
        c = pltpu.make_async_remote_copy(
            src_ref=src, dst_ref=dst, send_sem=red_send.at[k], recv_sem=red_recv.at[k],
            device_id=peer, device_id_type=MESH,
        )
        c.start()
        return c

    def piece(m):
        return pl.ds(pl.multiple_of(m * chunk, chunk), chunk)

    copies = []
    for d in range(1, nm):
        copies.append(reduce_copy(d, payload.at[piece((member + d) % nm)], rs_buf.at[member], in_team(d)))
    rs_buf[member] = payload[piece(member)]
    for c in copies:
        c.wait()

    def ordered_sum(buf, n):
        total = buf[0]
        for i in range(1, n):
            total = total + buf[i]
        return total

    y_buf[yy] = ordered_sum(rs_buf, nm)
    copies = [reduce_copy(nm + d, y_buf.at[yy], y_buf.at[yy], in_y(d)) for d in range(1, ny)]
    for c in copies:
        c.wait()
    z_buf[zz] = ordered_sum(y_buf, ny)
    copies = [reduce_copy(nm + ny + d, z_buf.at[zz], z_buf.at[zz], in_z(d)) for d in range(1, nz)]
    for c in copies:
        c.wait()
    full[piece(member)] = ordered_sum(z_buf, nz)
    copies = [
        reduce_copy(nm + ny + nz + d, full.at[piece(member)], full.at[piece(member)], in_team(d))
        for d in range(1, nm)
    ]
    for c in copies:
        c.wait()

    g = full[...] * scale
    gb = g[0:nb]
    ap = g[nb : nb + hb]
    ga_rows = jnp.concatenate([gb, pltpu.roll(ap, nb, 1), ap], axis=0)
    wa = g[base : base + 2 * np_]
    ww = g[base + 2 * np_ : base + 4 * np_]
    w1a, w2a = wa[0:np_], wa[np_:]
    n2 = 2 * np_
    h1 = jnp.where(lane_low, w1a, 0.0)
    v_a = w1a - small_dot(h1[:, 0:nb], gb, NN)
    v_w = ww[0:np_, 0:n2] - small_dot(h1, wa, NT)
    gram = v_w[:, 0:np_] - small_dot(v_a, h1, NT)
    lt1, li1 = eliminate(gram)
    t_b = -small_dot(li1, h1, NN)
    t_a = small_dot(li1, v_a, NN)
    t_w = small_dot(li1, v_w, NN)
    u_a = pltpu.roll(t_b, nb, 1)
    gu_a = small_dot(u_a, ga_rows, NT) + small_dot(li1, w2a, NN)
    gu_w = small_dot(u_a, wa, NT) + small_dot(li1, ww[np_:, 0:n2], NN)
    h2b = jnp.where(lane_low, gu_a, 0.0)
    h2q = small_dot(h2b, t_b, NT) + small_dot(gu_w[:, 0:np_], li1, NT)
    c2a = u_a - h2b - small_dot(h2q, t_b, NN)
    c2w = -small_dot(h2q, li1, NN)
    g2a = gu_a - small_dot(h2b[:, 0:nb], gb, NN) - small_dot(h2q, t_a, NN)
    g2w = gu_w - small_dot(h2b, wa, NT) - small_dot(h2q, t_w, NN)
    gram = small_dot(c2a, g2a, NT) + small_dot(c2w, g2w[:, 0:np_], NT) + small_dot(li1, g2w[:, np_:], NT)
    lt2, li2 = eliminate(gram)
    d_a = small_dot(li2, c2a, NN)
    d_w = small_dot(li2, c2w, NN)
    d_v = small_dot(li2, li1, NN)
    zero = jnp.zeros((np_, np_), F32)
    coef_a = jnp.concatenate([t_b, d_a], axis=0)
    coef_w = jnp.concatenate(
        [jnp.concatenate([li1, zero], axis=1), jnp.concatenate([d_w, d_v], axis=1)], axis=0
    )
    coef = jnp.concatenate([coef_a, coef_w], axis=1)
    c_hi, c_mid = split_two(coef)
    c_lo = (coef - c_hi.astype(F32) - c_mid.astype(F32)).astype(BF16)
    three = jnp.concatenate([c_hi, c_mid, c_lo], axis=0)
    two = jnp.concatenate([c_hi, c_mid], axis=0)
    width = min(512, end)

    def last_step(k, _):
        at = pl.ds(pl.multiple_of(k * width, width), width)
        o = lax.dot_general(three, z2[0:nt, at], NN, preferred_element_type=F32)
        p = lax.dot_general(two, z2[nt : 2 * nt, at], NN, preferred_element_type=F32)
        out = o[0:n2] + ((o[n2 : 2 * n2] + p[0:n2]) + (o[2 * n2 :] + p[n2:]))
        q1_ref[:, at] = out[0:np_]
        q2_ref[:, at] = out[np_:]
        return 0

    lax.fori_loop(0, end // width, last_step, 0)
    co_ref[0:np_] = h1
    co_ref[np_:n2] = h2b
    pad = jnp.zeros((np_, LANES - np_), F32)
    lt_ref[0:np_] = jnp.concatenate([lt1, pad], axis=1)
    lt_ref[np_:n2] = jnp.concatenate([lt2, pad], axis=1)
    lt_ref[n2 : n2 + np_] = jnp.concatenate([h2q, pad], axis=1)


def local(nz, nx, ny, basis, panel, rate_codes):
    nb, rows, width = basis.shape
    np_ = panel.shape[0]
    sites = rows * width * nz * nx * ny * 2
    nc, nt, flat, nm = nb + np_, 2 * nb + 2 * np_, rows * width, nx * 2
    dims = (nz, nx, ny, rows, nb, np_, 1.0 / sites)
    vm = pltpu.VMEM
    tile = lambda n: vm((n, LANES), F32)
    scratch = [
        vm((5, rows, LANES), F32),
        tile(nc), tile(nc), vm((8, LANES), jnp.int32), vm((8, LANES), jnp.int32),
        tile(nc), tile(nc), tile(nc), tile(nc),
        vm((np_, flat), F32), tile(np_), tile(np_), tile(np_), tile(np_), tile(np_), tile(np_),
        vm((2 * nt, flat), BF16), vm((2 * nt, nt), F32),
        tile(128), vm((nm, 128 // nm, LANES), F32), vm((ny, 128 // nm, LANES), F32),
        vm((nz, 128 // nm, LANES), F32), tile(128),
        pltpu.SemaphoreType.DMA((14,)), pltpu.SemaphoreType.DMA((14,)),
        pltpu.SemaphoreType.DMA((2 * nm + ny + nz,)), pltpu.SemaphoreType.DMA((2 * nm + ny + nz,)),
    ]
    spec = pl.BlockSpec(memory_space=pltpu.VMEM)
    q1, q2, co, lt = pl.pallas_call(
        functools.partial(kernel, dims),
        out_shape=(
            jax.ShapeDtypeStruct((np_, flat), F32),
            jax.ShapeDtypeStruct((np_, flat), F32),
            jax.ShapeDtypeStruct((2 * np_, LANES), F32),
            jax.ShapeDtypeStruct((3 * np_, LANES), F32),
        ),
        in_specs=[spec] * 3,
        out_specs=(spec,) * 4,
        scratch_shapes=scratch,
        compiler_params=pltpu.CompilerParams(collective_id=0, has_side_effects=True, vmem_limit_bytes=32 << 20),
        cost_estimate=pl.CostEstimate(flops=10**9, bytes_accessed=4 << 20, transcendentals=0),
    )(basis.reshape(nb, flat), panel.reshape(np_, flat), rate_codes)
    first = jnp.concatenate([co[0:np_, 0:nb].T, lt[0:np_, 0:np_]], axis=0)
    second = jnp.concatenate(
        [co[np_:, 0:nb].T, lt[2 * np_ :, 0:np_].T, lt[np_ : 2 * np_, 0:np_]], axis=0
    )
    return (q1.reshape(np_, rows, width), q2.reshape(np_, rows, width), first, second)


def solution(mesh):
    nx = 4
    nz = mesh.shape["gx"] // nx
    ny = mesh.shape["gy"] // 2
    placed = P(None, "gx", "gy")
    return jax.shard_map(
        functools.partial(local, nz, nx, ny),
        mesh=mesh,
        in_specs=(placed, placed, placed),
        out_specs=(placed, placed, P(), P()),
        check_vma=False,
    )
```

time: 142 us -> 66.5 us (0.47)
  Pallas kernels: 0 us -> 58.7 us
  blocking collectives: 53.1 us -> 0 us
  starting transfers between devices: 34.7 us -> 0 us
  waiting for transfers between devices: 23.6 us -> 0 us
  matrix products: 13.2 us -> 0 us
  other arithmetic: 10.3 us -> 1.34 us
    pallas_call x0 -> x1, Pallas kernels: none -> 58.7 us  [local(): pl.pallas_call(functools.partial(kernel, dims), out_shape=(jax.ShapeDtype...]
    all_to_all x2 -> x0, blocking collectives: 53.1 us -> none  [from_everyone(): lax.all_to_all(jnp.broadcast_to(array[None], (count, *array.shape)), axis...]
    ppermute x8 -> x0, starting transfers between devices: 21.8 us -> none  [from_behind(): return lax.ppermute(block, axis, route)]
    all_to_all x2 -> x0, waiting for transfers between devices: 15.5 us -> none  [from_everyone(): lax.all_to_all(jnp.broadcast_to(array[None], (count, *array.shape)), axis...]
    all_to_all x2 -> x0, starting transfers between devices: 12.9 us -> none  [from_everyone(): lax.all_to_all(jnp.broadcast_to(array[None], (count, *array.shape)), axis...]
    dot_general x17 -> x0, matrix products: 12.8 us -> none  [the longest x2 5.06 us: finish(): cleaned = image - jnp.dot(proj_coef.T, space, precision=HIGH)]
    ppermute x8 -> x0, waiting for transfers between devices: 8.16 us -> none  [from_behind(): return lax.ppermute(block, axis, route)]
    another operation x8 -> x0, other arithmetic: 4.06 us -> none  [the longest x6 2.81 us: finish(): lower_fac = jnp.linalg.cholesky(gram_mat)]
  transfers between devices with their start and end apart: 10 -> 0, of which waited for: 5 -> 0; matrix products, arithmetic and copies ran while one was open for 2% -> 0% of each run, Pallas kernels for 0% -> 0%
where the time goes in v1:
time: 66.5 us; the launch traced here: 66.3 us
  Pallas kernels  58.7 us (88%)
  local copies, waits for them, and re-layouts  5.58 us (8%)
  other arithmetic  1.34 us (2%)
    pallas_call x1, Pallas kernels, local(): pl.pallas_call(functools.partial(kernel, dims), out_shape=(jax.ShapeDtype...  58.7 us
    unnamed x6, local copies, waits for them, and re-layouts  5.44 us

profile of v1, /device:TPU:1, one launch (start us, length us, event | category | flops | bytes accessed | tf_op | source)
XLA Modules:
  0.0 66.3 jit_solution(3424350605197065801)
XLA Ops:
  0.6 1.1 %copy.16 = f32[1,8,64,128]{3,1,2,0:T(8,128)S(1)} copy(f32[1,8,64,128]{3,2,1,0:T(8,128)} %bitcast.21) | data formatting | bytes 524288
  1.7 0.0 copy-start
  1.8 2.8 %copy.15 = f32[8,8,64,128]{3,1,2,0:T(8,128)S(1)} copy(f32[8,8,64,128]{3,2,1,0:T(8,128)} %bitcast.20) | data formatting | bytes 4194304
  4.6 0.0 copy-done
  4.6 58.7 %shard_map.66 = (f32[8,8192]{1,0:T(8,128)S(1)}, f32[8,8192]{1,0:T(8,128)S(1)}, f32[16,128]{1,0:T(8,128)S(1)}, f32[24,128]{1,0:T(8,128)S(1)}) custom-call(f32[64,8192]{1,0:T(8,128)S(1)} %bitcast.16, f32[8,8192]{1,0:T(8,128)S(1)} %bitcast.19, s32[4,64,128]{2,1,0:T(8,128)S(1)} %copy-done), custom_call_target="tpu_custom_call" | custom-call | flops 1000000000 | bytes 4194304 | tf_op jit(solution)/shard_map/pallas_call | solution.py:389
  63.3 0.8 %copy.9 = f32[8,64,128]{2,1,0:T(8,128)} copy(f32[8,64,128]{2,0,1:T(8,128)S(1)} %bitcast.18) | data formatting | bytes 524288
  64.1 0.8 %copy.10 = f32[8,64,128]{2,1,0:T(8,128)} copy(f32[8,64,128]{2,0,1:T(8,128)S(1)} %bitcast.17) | data formatting | bytes 524288
  64.8 0.1 copy.8
  64.9 0.7 %pad_maximum_fusion.1 = f32[80,8]{0,1:T(8,128)} fusion(f32[8,8]{0,1:T(8,128)S(1)} %copy.8, f32[8,8]{0,1:T(8,128)S(1)} %get-tuple-element.16, f32[64,8]{0,1:T(8,128)S(1)} %get-tuple-element.19), kind=kLoop, calls=%fused_computation.3 | loop fusion | flops 1280 | bytes 5120 | tf_op jit(solution)/shard_map/concatenate | solution.py:404
  65.6 0.1 copy.7
  65.7 0.7 %pad_maximum_fusion = f32[72,8]{0,1:T(8,128)} fusion(f32[8,8]{0,1:T(8,128)S(1)} %copy.7, f32[64,8]{0,1:T(8,128)S(1)} %get-tuple-element.20), kind=kLoop, calls=%fused_computation.2 | loop fusion | flops 576 | bytes 4608 | tf_op jit(solution)/shard_map/concatenate | solution.py:403
  (2 shorter events, 0.0 us)
Async XLA Ops:
  1.7 2.8 %copy-start = (s32[4,64,128]{2,1,0:T(8,128)S(1)}, s32[4,64,128]{2,1,0:T(8,128)}, u32[]{:S(2)}) copy-start(s32[4,64,128]{2,1,0:T(8,128)} %codes_ref.1) | copy-start | bytes 393220

commit v2 on v1

v2 whole, which is shorter than its diff:
```python
import functools

import jax
import jax.numpy as jnp
from jax import lax
from jax.experimental import pallas as pl
from jax.experimental.pallas import tpu as pltpu
from jax.sharding import PartitionSpec as P

HIGH = lax.Precision.HIGHEST
MESH = pl.DeviceIdType.MESH
F32 = jnp.float32
BF16 = jnp.bfloat16
NN = (((1,), (0,)), ((), ()))
NT = (((1,), (1,)), ((), ()))
LANES = 128


def small_dot(a, b, dims):
    return lax.dot_general(a, b, dims, precision=HIGH, preferred_element_type=F32)


def split_two(x):
    hi = x.astype(BF16)
    lo = (x - hi.astype(F32)).astype(BF16)
    return hi, lo


def eliminate(gram):
    n = gram.shape[0]
    row = lax.broadcasted_iota(jnp.int32, (n, n), 0)
    col = lax.broadcasted_iota(jnp.int32, (n, n), 1)
    left = gram
    right = jnp.where(row == col, 1.0, 0.0).astype(F32)
    for j in range(n):
        factor = jnp.where(row[:, :1] > j, left[:, j : j + 1] / left[j : j + 1, j : j + 1], 0.0)
        left, right = (left - factor * left[j : j + 1, :], right - factor * right[j : j + 1, :])
    diag = jnp.sum(jnp.where(row == col, left, 0.0), axis=1, keepdims=True)
    root = 1.0 / jnp.sqrt(diag)
    return jnp.where(row <= col, left * root, 0.0), right * root


def kernel(
    dims,
    b_hbm, p_hbm, codes_hbm,
    q1_ref, q2_ref, c1_ref, c2_ref,
    xt, wt, codes, rf, up_r, dn_r, pack_l, pack_r, from_l, from_r, wpack_l, wpack_r, wfrom_l, wfrom_r,
    z2, acc, payload, rs_buf, a_buf, b_buf, full,
    load_sem, halo_send, halo_recv, red_send, red_recv,
):
    nz, nx, ny, rows, nb, np_, scale = dims
    nm = nx * 2
    gx, gy = lax.axis_index("gx"), lax.axis_index("gy")
    zz, xx = gx // nx, gx % nx
    yy, core = gy // 2, gy % 2
    member = xx * 2 + core
    ngx, ngy = nz * nx, ny * 2
    above = ((gx + ngx - 1) % ngx, gy)
    below = ((gx + 1) % ngx, gy)
    left = (gx, (gy + ngy - 1) % ngy)
    right = (gx, (gy + 1) % ngy)

    def in_team(d):
        m = (member + d) % nm
        return (zz * nx + m // 2, yy * 2 + m % 2)

    def in_y(d):
        return (gx, ((yy + d) % ny) * 2 + core)

    def in_z(d):
        return (((zz + d) % nz) * nx + xx, gy)

    def in_first(d):
        a, b = in_y(d), in_z(d)
        return (a[0] * (1 - core) + b[0] * core, a[1] * (1 - core) + b[1] * core)

    def in_second(d):
        a, b = in_z(d), in_y(d)
        return (a[0] * (1 - core) + b[0] * core, a[1] * (1 - core) + b[1] * core)

    peers = [above, below, left, right]
    peers += [in_team(d) for d in range(1, nm)]
    peers += [in_y(d) for d in range(1, ny)]
    peers += [in_z(d) for d in range(1, nz)]
    barrier = pltpu.get_barrier_semaphore()
    for peer in peers:
        pl.semaphore_signal(barrier, inc=1, device_id=peer, device_id_type=MESH)

    nc = nb + np_
    nt = nb * 2 + np_ * 2
    inner = slice(1, rows + 1)
    load_codes = pltpu.make_async_copy(codes_hbm, codes, load_sem.at[0])
    load_codes.start()
    for c in range(np_):
        pltpu.make_async_copy(p_hbm.at[c], xt.at[inner, nb + c], load_sem.at[1]).start()
    for c in range(nb):
        pltpu.make_async_copy(b_hbm.at[c], xt.at[inner, c], load_sem.at[2]).start()

    lane = lax.broadcasted_iota(jnp.int32, (1, LANES), 1)
    top = 8

    def rate(d, r):
        return rf[d, pl.ds(r + top, 1), :]

    def pack_step(x, r, accs):
        y = jnp.where(lane == LANES - 1, rate(3, r) * x, rate(2, r) * x)
        y = pltpu.roll(y, r, 1)
        a, b = accs
        return (jnp.where(lane == r, y, a), jnp.where(lane == (r + LANES - 1) % LANES, y, b))

    def pack(at, n):
        per = 8

        def body(k, accs):
            for i in range(per):
                accs = pack_step(xt[k * per + i + 1, at], k * per + i, accs)
            return accs

        zero = jnp.zeros((n, LANES), F32)
        a, b = lax.fori_loop(0, rows // per, body, (zero, zero))
        pack_l[at] = a
        pack_r[at] = b

    load_codes.wait()
    values = codes[...].astype(F32) * 0.125
    rf[0:4, top : top + rows] = values
    rf[4, top : top + rows] = values[0] + values[1] + values[2] + values[3]
    pltpu.make_async_copy(p_hbm, xt.at[inner, nb:nc], load_sem.at[1]).wait()
    pack(slice(nb, nc), np_)

    pl.semaphore_wait(barrier, len(peers))

    def halo(k, src, dst, peer):
        c = pltpu.make_async_remote_copy(
            src_ref=src, dst_ref=dst, send_sem=halo_send.at[k], recv_sem=halo_recv.at[k],
            device_id=peer, device_id_type=MESH,
        )
        c.start()
        return c

    small = [
        halo(0, xt.at[rows, nb:nc], xt.at[0, nb:nc], below),
        halo(1, xt.at[1, nb:nc], xt.at[rows + 1, nb:nc], above),
        halo(2, pack_r.at[nb:nc], from_l.at[nb:nc], right),
        halo(3, pack_l.at[nb:nc], from_r.at[nb:nc], left),
        halo(4, codes.at[1, rows - 8 : rows], up_r, below),
        halo(5, codes.at[0, 0:8], dn_r, above),
    ]
    pltpu.make_async_copy(b_hbm, xt.at[inner, 0:nb], load_sem.at[2]).wait()
    big = [
        halo(6, xt.at[rows, 0:nb], xt.at[0, 0:nb], below),
        halo(7, xt.at[1, 0:nb], xt.at[rows + 1, 0:nb], above),
    ]
    pack(slice(0, nb), nb)
    big += [
        halo(8, pack_r.at[0:nb], from_l.at[0:nb], right),
        halo(9, pack_l.at[0:nb], from_r.at[0:nb], left),
    ]

    def put(first, r, x):
        hi, lo = split_two(x)
        at = pl.ds(pl.multiple_of(r * LANES, LANES), LANES)
        z2[first : first + x.shape[0], at] = hi
        z2[nt + first : nt + first + x.shape[0], at] = lo

    def split_b(k, _):
        for i in range(2):
            put(0, 2 * k + i, xt[2 * k + i + 1, 0:nb])
        return 0

    lax.fori_loop(0, rows // 2, split_b, 0)

    def stencil(r, xu, x, xd, fl, fr):
        from_l = jnp.where(lane == 0, pltpu.roll(fl, (2 * LANES + 1 - r) % LANES, 1), pltpu.roll(rate(3, r) * x, 1, 1))
        from_r = jnp.where(
            lane == LANES - 1, pltpu.roll(fr, (2 * LANES - 1 - r) % LANES, 1), pltpu.roll(rate(2, r) * x, LANES - 1, 1)
        )
        return (rate(1, r - 1) * xu + rate(0, r + 1) * xd) + (from_l + from_r) - rate(4, r) * x

    def sweep(x_at, fl, fr, emit, carry, per):
        def body(k, c):
            rs = [k * per + i for i in range(per)]
            outs = [stencil(r, x_at(r - 1), x_at(r), x_at(r + 1), fl, fr) for r in rs]
            for r, out in zip(rs, outs):
                c = emit(r, out, c)
            return c

        return lax.fori_loop(0, rows // per, body, carry)

    def present(k):
        return jnp.where(k, 1.0, 0.0).astype(F32)

    has_l, has_r = present(gy > 0), present(gy < ngy - 1)
    for c in small:
        c.wait()
    rf[1, top - 1 : top] = up_r[7:8].astype(F32) * 0.125 * present(gx > 0)
    rf[0, top + rows : top + rows + 1] = dn_r[0:1].astype(F32) * 0.125 * present(gx < ngx - 1)

    def emit_w(r, out, accs):
        wt[r + 1] = out
        return pack_step(out, r, accs)

    zp = jnp.zeros((np_, LANES), F32)
    a, b = sweep(lambda r: xt[r + 1, nb:nc], from_l[nb:nc] * has_l, from_r[nb:nc] * has_r, emit_w, (zp, zp), 16)
    wpack_l[...] = a
    wpack_r[...] = b
    wsend = [
        halo(10, wt.at[rows], wt.at[0], below),
        halo(11, wt.at[1], wt.at[rows + 1], above),
        halo(12, wpack_r, wfrom_l, right),
        halo(13, wpack_l, wfrom_r, left),
    ]

    for c in big:
        c.wait()

    def emit_b(r, out, c):
        put(nb, r, out)
        return c

    sweep(lambda r: xt[r + 1, 0:nb], from_l[0:nb] * has_l, from_r[0:nb] * has_r, emit_b, 0, 2)

    for c in wsend:
        c.wait()

    def emit_aw(r, out, c):
        put(2 * nb, r, jnp.concatenate([wt[r + 1], out], axis=0))
        return c

    sweep(lambda r: wt[r + 1], wfrom_l[...] * has_l, wfrom_r[...] * has_r, emit_aw, 0, 16)

    end = rows * LANES
    step = min(1024, end)
    acc[...] = jnp.zeros_like(acc)

    def gram_step(k, _):
        at = pl.ds(pl.multiple_of(k * step, step), step)
        acc[...] += lax.dot_general(z2[:, at], z2[0:nt, at], NT, preferred_element_type=F32)
        return 0

    lax.fori_loop(0, end // step, gram_step, 0)
    na, n2 = 2 * nb, 2 * np_
    half = acc[0:nt, :] * 0.5 + acc[nt : 2 * nt, :]
    aa = half[0:na, 0:na]
    aa = aa + aa.T
    aw = jnp.concatenate([half[0:na, na:nt], jnp.zeros((na, LANES - n2), F32)], axis=1)
    wa = half[na:nt, 0:na] + aw.T[0:n2, :]
    ww = half[na:nt, na:nt]
    ww = ww + ww.T
    low = lane < nb
    site = lax.broadcasted_iota(jnp.int32, (nb, LANES), 0)
    upper, same = lane >= site, lane == site
    ab_ab = pltpu.roll(aa[nb:na], nb, 1)
    main = jnp.where(low & ~upper, ab_ab, aa[0:nb])
    diag = jnp.sum(jnp.where(same, ab_ab, 0.0), axis=0, keepdims=True)
    extra = jnp.concatenate(
        [
            wa,
            jnp.concatenate([ww[0:np_], ww[np_:n2], jnp.zeros((np_, LANES - 2 * n2), F32)], axis=1),
            jnp.broadcast_to(diag, (8, LANES)),
        ],
        axis=0,
    )
    per_main, per_extra = nb // nm, 32 // nm
    per_all = per_main + per_extra
    for m in range(nm):
        payload[m, 0:per_main] = main[m * per_main : (m + 1) * per_main]
        payload[m, per_main:per_all] = extra[m * per_extra : (m + 1) * per_extra]

    def reduce_copy(k, src, dst, peer):
        c = pltpu.make_async_remote_copy(
            src_ref=src.at[0:per_all], dst_ref=dst.at[0:per_all], send_sem=red_send.at[k], recv_sem=red_recv.at[k],
            device_id=peer, device_id_type=MESH,
        )
        c.start()
        return c

    copies = []
    for d in range(1, nm):
        copies.append(reduce_copy(d, payload.at[(member + d) % nm], rs_buf.at[member], in_team(d)))
    rs_buf[member, 0:per_all] = payload[member, 0:per_all]
    for c in copies:
        c.wait()

    def ordered_sum(buf, n):
        total = buf[0, 0:per_all]
        for i in range(1, n):
            total = total + buf[i, 0:per_all]
        return total

    one = yy * (1 - core) + zz * core
    two = zz * (1 - core) + yy * core
    a_buf[one, 0:per_all] = ordered_sum(rs_buf, nm)
    copies = [reduce_copy(nm + d, a_buf.at[one], a_buf.at[one], in_first(d)) for d in range(1, ny)]
    for c in copies:
        c.wait()
    b_buf[two, 0:per_all] = ordered_sum(a_buf, ny)
    copies = [reduce_copy(nm + ny + d, b_buf.at[two], b_buf.at[two], in_second(d)) for d in range(1, nz)]
    for c in copies:
        c.wait()
    full[member, 0:per_all] = ordered_sum(b_buf, nz)
    copies = [
        reduce_copy(nm + ny + nz + d, full.at[member], full.at[member], in_team(d)) for d in range(1, nm)
    ]
    for c in copies:
        c.wait()

    main = jnp.concatenate([full[m, 0:per_main] for m in range(nm)], axis=0) * scale
    extra = jnp.concatenate([full[m, per_main:per_all] for m in range(nm)], axis=0) * scale
    wa = extra[0:n2]
    ww = extra[n2 : n2 + np_]
    diag = extra[n2 + np_ : n2 + np_ + 1]
    square = jnp.where(low, main, 0.0)
    flip = jnp.concatenate([square, jnp.zeros_like(square)], axis=0).T[0:nb]
    gb = jnp.where(low & ~upper, flip, main)
    ab_ab = jnp.where(low, jnp.where(upper, jnp.where(same, diag, flip), square), 0.0)
    ga_rows = jnp.concatenate([gb, pltpu.roll(ab_ab, nb, 1)], axis=0)
    w1a, w2a = wa[0:np_], wa[np_:]
    h1 = jnp.where(low, w1a, 0.0)
    v_a = w1a - small_dot(h1[:, 0:nb], gb, NN)
    v_w = ww[:, 0:n2] - small_dot(h1, wa, NT)
    gram = v_w[:, 0:np_] - small_dot(v_a, h1, NT)
    lt1, li1 = eliminate(gram)
    t_b = -small_dot(li1, h1, NN)
    t_a = small_dot(li1, v_a, NN)
    t_w = small_dot(li1, v_w, NN)
    u_a = pltpu.roll(t_b, nb, 1)
    gu_a = small_dot(u_a, ga_rows, NT) + small_dot(li1, w2a, NN)
    gu_w = small_dot(u_a, wa, NT) + small_dot(li1, ww[:, n2 : 2 * n2], NN)
    h2b = jnp.where(low, gu_a, 0.0)
    h2q = small_dot(h2b, t_b, NT) + small_dot(gu_w[:, 0:np_], li1, NT)
    c2a = u_a - h2b - small_dot(h2q, t_b, NN)
    c2w = -small_dot(h2q, li1, NN)
    g2a = gu_a - small_dot(h2b[:, 0:nb], gb, NN) - small_dot(h2q, t_a, NN)
    g2w = gu_w - small_dot(h2b, wa, NT) - small_dot(h2q, t_w, NN)
    gram = small_dot(c2a, g2a, NT) + small_dot(c2w, g2w[:, 0:np_], NT) + small_dot(li1, g2w[:, np_:], NT)
    lt2, li2 = eliminate(gram)
    d_a = small_dot(li2, c2a, NN)
    d_w = small_dot(li2, c2w, NN)
    d_v = small_dot(li2, li1, NN)
    zero = jnp.zeros((np_, np_), F32)
    coef_a = jnp.concatenate([t_b, d_a], axis=0)
    coef_w = jnp.concatenate(
        [jnp.concatenate([li1, zero], axis=1), jnp.concatenate([d_w, d_v], axis=1)], axis=0
    )
    coef = jnp.concatenate([coef_a, coef_w], axis=1)
    c_hi, c_mid = split_two(coef)
    c_lo = (coef - c_hi.astype(F32) - c_mid.astype(F32)).astype(BF16)
    three = jnp.concatenate([c_hi, c_mid, c_lo], axis=0)
    pair = jnp.concatenate([c_hi, c_mid], axis=0)
    per = min(4, rows)
    width = per * LANES

    def last_step(k, _):
        at = pl.ds(pl.multiple_of(k * width, width), width)
        o = lax.dot_general(three, z2[0:nt, at], NN, preferred_element_type=F32)
        p = lax.dot_general(pair, z2[nt : 2 * nt, at], NN, preferred_element_type=F32)
        out = o[0:n2] + ((o[n2 : 2 * n2] + p[0:n2]) + (o[2 * n2 :] + p[n2:]))
        for i in range(per):
            q1_ref[:, k * per + i, :] = out[0:np_, i * LANES : (i + 1) * LANES]
            q2_ref[:, k * per + i, :] = out[np_:, i * LANES : (i + 1) * LANES]
        return 0

    lax.fori_loop(0, rows // per, last_step, 0)

    def placed(x, first):
        wide = jnp.concatenate([x, jnp.zeros((np_, LANES - np_), F32)], axis=1)
        return pltpu.roll(wide, first, 1)

    c1_ref[...] = (h1 + placed(lt1.T, nb))[:, 0:nc]
    c2_ref[...] = (h2b + placed(h2q, nb) + placed(lt2.T, nc))[:, 0 : nc + np_]


def local(nz, nx, ny, basis, panel, rate_codes):
    nb, rows, width = basis.shape
    np_ = panel.shape[0]
    sites = rows * width * nz * nx * ny * 2
    nc, nt, flat, nm = nb + np_, 2 * nb + 2 * np_, rows * width, nx * 2
    dims = (nz, nx, ny, rows, nb, np_, 1.0 / sites)
    vm = pltpu.VMEM
    tile = lambda *n: vm((*n, LANES), F32)
    dma = pltpu.SemaphoreType.DMA
    scratch = [
        tile(rows + 2, nc), tile(rows + 2, np_), vm((4, rows, LANES), jnp.int32), tile(5, rows + 16),
        vm((8, LANES), jnp.int32), vm((8, LANES), jnp.int32),
        tile(nc), tile(nc), tile(nc), tile(nc), tile(np_), tile(np_), tile(np_), tile(np_),
        vm((2 * nt, flat), BF16), vm((2 * nt, nt), F32),
        tile(nm, 16), tile(nm, 16), tile(ny, 16), tile(nz, 16), tile(nm, 16),
        dma((3,)), dma((14,)), dma((14,)), dma((2 * nm + ny + nz,)), dma((2 * nm + ny + nz,)),
    ]
    vmem = pl.BlockSpec(memory_space=pltpu.VMEM)
    q1, q2, c1, c2 = pl.pallas_call(
        functools.partial(kernel, dims),
        out_shape=(
            jax.ShapeDtypeStruct((np_, rows, width), F32),
            jax.ShapeDtypeStruct((np_, rows, width), F32),
            jax.ShapeDtypeStruct((np_, nc), F32),
            jax.ShapeDtypeStruct((np_, nc + np_), F32),
        ),
        in_specs=[pl.BlockSpec(memory_space=pltpu.HBM)] * 3,
        out_specs=(vmem,) * 4,
        scratch_shapes=scratch,
        compiler_params=pltpu.CompilerParams(collective_id=0, has_side_effects=True, vmem_limit_bytes=48 << 20),
        cost_estimate=pl.CostEstimate(flops=10**9, bytes_accessed=4 << 20, transcendentals=0),
    )(*[pltpu.with_memory_space_constraint(v, pltpu.HBM) for v in (basis, panel, rate_codes)])
    return (q1, q2, c1.T, c2.T)


def solution(mesh):
    nx = 4
    nz = mesh.shape["gx"] // nx
    ny = mesh.shape["gy"] // 2
    placed = P(None, "gx", "gy")
    return jax.shard_map(
        functools.partial(local, nz, nx, ny),
        mesh=mesh,
        in_specs=(placed, placed, placed),
        out_specs=(placed, placed, P(), P()),
        check_vma=False,
    )
```

time: 66.5 us -> 57.5 us (0.86)
  Pallas kernels: 58.7 us -> 54.1 us
  local copies, waits for them, and re-layouts: 5.58 us -> 2.59 us
  other arithmetic: 1.34 us -> 0 us
    pallas_call x1, Pallas kernels: 58.7 us -> 54.1 us  [local(): pl.pallas_call(functools.partial(kernel, dims), out_shape=(jax.ShapeDtype...]
    unnamed x6 -> x4, local copies, waits for them, and re-layouts: 5.44 us -> 2.59 us
    concatenate x2 -> x0, other arithmetic: 1.34 us -> none  [the longest x1 0.67 us: local(): jnp.concatenate([co[np_:, 0:nb].T, lt[2 * np_:, 0:np_].T, lt[np_:2 * np_,...]
where the time goes in v2:
time: 57.5 us; the launch traced here: 57.3 us
  Pallas kernels  54.1 us (94%)
  local copies, waits for them, and re-layouts  2.59 us (5%)
  between operations  0.64 us (1%)
    pallas_call x1, Pallas kernels, local(): pl.pallas_call(functools.partial(kernel, dims), out_shape=(jax.ShapeDtype...  54.1 us
    unnamed x4, local copies, waits for them, and re-layouts  2.59 us

profile of v2, /device:TPU:1, one launch (start us, length us, event | category | flops | bytes accessed | tf_op | source)
XLA Modules:
  0.0 57.3 jit_solution(1292521186179335481)
XLA Ops:
  0.6 54.1 %shard_map.66 = (f32[8,64,128]{2,1,0:T(8,128)S(1)}, f32[8,64,128]{2,1,0:T(8,128)S(1)}, f32[8,72]{1,0:T(8,128)S(1)}, f32[8,80]{1,0:T(8,128)S(1)}) custom-call(f32[64,64,128]{2,1,0:T(8,128)} %b_hbm.1, f32[8,64,128]{2,1,0:T(8,128)} %p_hbm.1, s32[4,64,128]{2,1,0:T(8,128)} %codes_hbm.1), custom_call_target="tpu_custom_call" | custom-call | flops 1000000000 | bytes 4194304 | tf_op jit(solution)/shard_map/pallas_call | solution.py:392
  54.7 0.7 %copy.11 = f32[8,64,128]{2,1,0:T(8,128)} copy(f32[8,64,128]{2,1,0:T(8,128)S(1)} %get-tuple-element.16) | data formatting | bytes 524288
  55.4 0.7 %copy.12 = f32[8,64,128]{2,1,0:T(8,128)} copy(f32[8,64,128]{2,1,0:T(8,128)S(1)} %get-tuple-element.17) | data formatting | bytes 524288
  56.1 0.6 %copy.13 = f32[72,8]{0,1:T(8,128)} copy(f32[72,8]{0,1:T(8,128)S(1)} %bitcast.3) | data formatting | bytes 4608
  56.7 0.6 %copy.14 = f32[80,8]{0,1:T(8,128)} copy(f32[80,8]{0,1:T(8,128)S(1)} %bitcast.2) | data formatting | bytes 5120

commit v3 on v2

--- a/solution.py
+++ b/solution.py
@@ -45,7 +45,7 @@
     b_hbm, p_hbm, codes_hbm,
     q1_ref, q2_ref, c1_ref, c2_ref,
     xt, wt, codes, rf, up_r, dn_r, pack_l, pack_r, from_l, from_r, wpack_l, wpack_r, wfrom_l, wfrom_r,
-    z2, acc, payload, rs_buf, a_buf, b_buf, full,
+    part, z2, acc, accw, payload, rs_buf, a_buf, b_buf, full,
     load_sem, halo_send, halo_recv, red_send, red_recv,
 ):
     nz, nx, ny, rows, nb, np_, scale = dims
@@ -104,9 +104,9 @@
 
     def pack_step(x, r, accs):
         y = jnp.where(lane == LANES - 1, rate(3, r) * x, rate(2, r) * x)
-        y = pltpu.roll(y, r, 1)
+        y = pltpu.roll(y, 2 * r, 1)
         a, b = accs
-        return (jnp.where(lane == r, y, a), jnp.where(lane == (r + LANES - 1) % LANES, y, b))
+        return (jnp.where(lane == 2 * r, y, a), jnp.where(lane == (2 * r + LANES - 1) % LANES, y, b))
 
     def pack(at, n):
         per = 8
@@ -157,36 +157,48 @@
         halo(9, pack_l.at[0:nb], from_r.at[0:nb], left),
     ]
 
+    na, n2 = 2 * nb, 2 * np_
+
+    def at_row(r):
+        return pl.ds(pl.multiple_of(r * LANES, LANES), LANES)
+
     def put(first, r, x):
         hi, lo = split_two(x)
-        at = pl.ds(pl.multiple_of(r * LANES, LANES), LANES)
-        z2[first : first + x.shape[0], at] = hi
-        z2[nt + first : nt + first + x.shape[0], at] = lo
-
-    def split_b(k, _):
-        for i in range(2):
-            put(0, 2 * k + i, xt[2 * k + i + 1, 0:nb])
+        z2[first : first + nb, at_row(r)] = hi
+        z2[na + first : na + first + nb, at_row(r)] = lo
+
+    def own(r, x):
+        from_l = jnp.where(lane == 0, 0.0, pltpu.roll(rate(3, r) * x, 1, 1))
+        from_r = jnp.where(lane == LANES - 1, 0.0, pltpu.roll(rate(2, r) * x, LANES - 1, 1))
+        return from_l + from_r - rate(4, r) * x
+
+    def other(r, xu, xd, sides):
+        side = pltpu.roll(sides, (2 * LANES - 1 - 2 * r) % LANES, 1)
+        return rate(1, r - 1) * xu + rate(0, r + 1) * xd + jnp.where((lane == 0) | (lane == LANES - 1), side, 0.0)
+
+    def own_step(k, _):
+        for i in range(4):
+            r = 4 * k + i
+            x = xt[r + 1, 0:nb]
+            put(0, r, x)
+            part[r] = own(r, x)
         return 0
 
-    lax.fori_loop(0, rows // 2, split_b, 0)
-
-    def stencil(r, xu, x, xd, fl, fr):
-        from_l = jnp.where(lane == 0, pltpu.roll(fl, (2 * LANES + 1 - r) % LANES, 1), pltpu.roll(rate(3, r) * x, 1, 1))
-        from_r = jnp.where(
-            lane == LANES - 1, pltpu.roll(fr, (2 * LANES - 1 - r) % LANES, 1), pltpu.roll(rate(2, r) * x, LANES - 1, 1)
-        )
-        return (rate(1, r - 1) * xu + rate(0, r + 1) * xd) + (from_l + from_r) - rate(4, r) * x
-
-    def sweep(x_at, fl, fr, emit, carry, per):
+    lax.fori_loop(0, rows // 4, own_step, 0)
+
+    def sweep(x_at, sides, emit, carry, per):
         def body(k, c):
             rs = [k * per + i for i in range(per)]
-            outs = [stencil(r, x_at(r - 1), x_at(r), x_at(r + 1), fl, fr) for r in rs]
+            outs = [own(r, x_at(r)) + other(r, x_at(r - 1), x_at(r + 1), sides) for r in rs]
             for r, out in zip(rs, outs):
                 c = emit(r, out, c)
             return c
 
         return lax.fori_loop(0, rows // per, body, carry)
 
+    def both_sides(fl, fr):
+        return jnp.where(lane % 2 == 0, fr * has_r, pltpu.roll(fl, 2, 1) * has_l)
+
     def present(k):
         return jnp.where(k, 1.0, 0.0).astype(F32)
 
@@ -201,7 +213,7 @@
         return pack_step(out, r, accs)
 
     zp = jnp.zeros((np_, LANES), F32)
-    a, b = sweep(lambda r: xt[r + 1, nb:nc], from_l[nb:nc] * has_l, from_r[nb:nc] * has_r, emit_w, (zp, zp), 16)
+    a, b = sweep(lambda r: xt[r + 1, nb:nc], both_sides(from_l[nb:nc], from_r[nb:nc]), emit_w, (zp, zp), 16)
     wpack_l[...] = a
     wpack_r[...] = b
     wsend = [
@@ -214,39 +226,57 @@
     for c in big:
         c.wait()
 
-    def emit_b(r, out, c):
-        put(nb, r, out)
-        return c
-
-    sweep(lambda r: xt[r + 1, 0:nb], from_l[0:nb] * has_l, from_r[0:nb] * has_r, emit_b, 0, 2)
-
-    for c in wsend:
-        c.wait()
-
-    def emit_aw(r, out, c):
-        put(2 * nb, r, jnp.concatenate([wt[r + 1], out], axis=0))
-        return c
-
-    sweep(lambda r: wt[r + 1], wfrom_l[...] * has_l, wfrom_r[...] * has_r, emit_aw, 0, 16)
+    sides_b = both_sides(from_l[0:nb], from_r[0:nb])
+
+    def other_step(k, _):
+        for i in range(4):
+            r = 4 * k + i
+            put(nb, r, part[r] + other(r, xt[r, 0:nb], xt[r + 2, 0:nb], sides_b))
+        return 0
+
+    lax.fori_loop(0, rows // 4, other_step, 0)
 
     end = rows * LANES
-    step = min(1024, end)
+    step = min(2048, end)
     acc[...] = jnp.zeros_like(acc)
 
     def gram_step(k, _):
         at = pl.ds(pl.multiple_of(k * step, step), step)
-        acc[...] += lax.dot_general(z2[:, at], z2[0:nt, at], NT, preferred_element_type=F32)
+        acc[...] += lax.dot_general(z2[0 : 2 * na, at], z2[0:na, at], NT, preferred_element_type=F32)
         return 0
 
     lax.fori_loop(0, end // step, gram_step, 0)
-    na, n2 = 2 * nb, 2 * np_
-    half = acc[0:nt, :] * 0.5 + acc[nt : 2 * nt, :]
-    aa = half[0:na, 0:na]
+
+    for c in wsend:
+        c.wait()
+
+    def emit_aw(r, out, c):
+        x = jnp.concatenate([wt[r + 1], out], axis=0)
+        hi, lo = split_two(x)
+        z2[2 * na : 2 * na + n2, at_row(r)] = hi
+        z2[2 * na + n2 : 2 * na + 2 * n2, at_row(r)] = lo
+        z2[2 * na + 2 * n2 :, at_row(r)] = (x - hi.astype(F32) - lo.astype(F32)).astype(BF16)
+        return c
+
+    sweep(lambda r: wt[r + 1], both_sides(wfrom_l[...], wfrom_r[...]), emit_aw, 0, 16)
+
+    accw[...] = jnp.zeros_like(accw)
+
+    def gram_w_step(k, _):
+        at = pl.ds(pl.multiple_of(k * step, step), step)
+        accw[...] += lax.dot_general(
+            z2[0 : 2 * na + 2 * n2, at], z2[2 * na : 2 * na + 2 * n2, at], NT, preferred_element_type=F32
+        )
+        return 0
+
+    lax.fori_loop(0, end // step, gram_w_step, 0)
+    aa = acc[0:na] * 0.5 + acc[na : 2 * na]
     aa = aa + aa.T
-    aw = jnp.concatenate([half[0:na, na:nt], jnp.zeros((na, LANES - n2), F32)], axis=1)
-    wa = half[na:nt, 0:na] + aw.T[0:n2, :]
-    ww = half[na:nt, na:nt]
-    ww = ww + ww.T
+    by_w = accw[...]
+    by_w = by_w[:, 0:n2] + by_w[:, n2 : 2 * n2]
+    aw = by_w[0:na] + by_w[na : 2 * na]
+    ww = by_w[2 * na : 2 * na + n2] + by_w[2 * na + n2 :]
+    wa = jnp.concatenate([aw, jnp.zeros((na, LANES - n2), F32)], axis=1).T[0:n2]
     low = lane < nb
     site = lax.broadcasted_iota(jnp.int32, (nb, LANES), 0)
     upper, same = lane >= site, lane == site
@@ -343,19 +373,26 @@
     coef_w = jnp.concatenate(
         [jnp.concatenate([li1, zero], axis=1), jnp.concatenate([d_w, d_v], axis=1)], axis=0
     )
-    coef = jnp.concatenate([coef_a, coef_w], axis=1)
-    c_hi, c_mid = split_two(coef)
-    c_lo = (coef - c_hi.astype(F32) - c_mid.astype(F32)).astype(BF16)
-    three = jnp.concatenate([c_hi, c_mid, c_lo], axis=0)
-    pair = jnp.concatenate([c_hi, c_mid], axis=0)
-    per = min(4, rows)
+    a_hi, a_mid = split_two(coef_a)
+    a_lo = (coef_a - a_hi.astype(F32) - a_mid.astype(F32)).astype(BF16)
+    w_hi, w_mid = split_two(coef_w)
+    w_lo = (coef_w - w_hi.astype(F32) - w_mid.astype(F32)).astype(BF16)
+    a_no, w_no = jnp.zeros_like(a_lo), jnp.zeros_like(w_lo)
+    three = jnp.concatenate(
+        [
+            jnp.concatenate([a_hi, a_hi, w_hi, w_hi, w_hi], axis=1),
+            jnp.concatenate([a_mid, a_mid, w_mid, w_mid, w_no], axis=1),
+            jnp.concatenate([a_lo, a_no, w_lo, w_no, w_no], axis=1),
+        ],
+        axis=0,
+    )
+    per = min(8, rows)
     width = per * LANES
 
     def last_step(k, _):
         at = pl.ds(pl.multiple_of(k * width, width), width)
-        o = lax.dot_general(three, z2[0:nt, at], NN, preferred_element_type=F32)
-        p = lax.dot_general(pair, z2[nt : 2 * nt, at], NN, preferred_element_type=F32)
-        out = o[0:n2] + ((o[n2 : 2 * n2] + p[0:n2]) + (o[2 * n2 :] + p[n2:]))
+        o = lax.dot_general(three, z2[:, at], NN, preferred_element_type=F32)
+        out = o[0:n2] + (o[n2 : 2 * n2] + o[2 * n2 :])
         for i in range(per):
             q1_ref[:, k * per + i, :] = out[0:np_, i * LANES : (i + 1) * LANES]
             q2_ref[:, k * per + i, :] = out[np_:, i * LANES : (i + 1) * LANES]
@@ -384,7 +421,7 @@
         tile(rows + 2, nc), tile(rows + 2, np_), vm((4, rows, LANES), jnp.int32), tile(5, rows + 16),
         vm((8, LANES), jnp.int32), vm((8, LANES), jnp.int32),
         tile(nc), tile(nc), tile(nc), tile(nc), tile(np_), tile(np_), tile(np_), tile(np_),
-        vm((2 * nt, flat), BF16), vm((2 * nt, nt), F32),
+        tile(rows, nb), vm((4 * nb + 6 * np_, flat), BF16), vm((4 * nb, 2 * nb), F32), vm((2 * nt, 4 * np_), F32),
         tile(nm, 16), tile(nm, 16), tile(ny, 16), tile(nz, 16), tile(nm, 16),
         dma((3,)), dma((14,)), dma((14,)), dma((2 * nm + ny + nz,)), dma((2 * nm + ny + nz,)),
     ]

time: 57.5 us -> 54.4 us (0.946)
  Pallas kernels: 54.1 us -> 51 us
    pallas_call x1, Pallas kernels: 54.1 us -> 51 us  [local(): pl.pallas_call(functools.partial(kernel, dims), out_shape=(jax.ShapeDtype...]
where the time goes in v3:
time: 54.4 us; the launch traced here: 54.3 us
  Pallas kernels  51 us (94%)
  local copies, waits for them, and re-layouts  2.59 us (5%)
  between operations  0.64 us (1%)
    pallas_call x1, Pallas kernels, local(): pl.pallas_call(functools.partial(kernel, dims), out_shape=(jax.ShapeDtype...  51 us
    unnamed x4, local copies, waits for them, and re-layouts  2.59 us

profile of v3, /device:TPU:1, one launch (start us, length us, event | category | flops | bytes accessed | tf_op | source)
XLA Modules:
  0.0 54.3 jit_solution(3237854185078040885)
XLA Ops:
  0.6 51.0 %shard_map.66 = (f32[8,64,128]{2,1,0:T(8,128)S(1)}, f32[8,64,128]{2,1,0:T(8,128)S(1)}, f32[8,72]{1,0:T(8,128)S(1)}, f32[8,80]{1,0:T(8,128)S(1)}) custom-call(f32[64,64,128]{2,1,0:T(8,128)} %b_hbm.1, f32[8,64,128]{2,1,0:T(8,128)} %p_hbm.1, s32[4,64,128]{2,1,0:T(8,128)} %codes_hbm.1), custom_call_target="tpu_custom_call" | custom-call | flops 1000000000 | bytes 4194304 | tf_op jit(solution)/shard_map/pallas_call | solution.py:429
  51.7 0.7 %copy.11 = f32[8,64,128]{2,1,0:T(8,128)} copy(f32[8,64,128]{2,1,0:T(8,128)S(1)} %get-tuple-element.16) | data formatting | bytes 524288
  52.4 0.7 %copy.12 = f32[8,64,128]{2,1,0:T(8,128)} copy(f32[8,64,128]{2,1,0:T(8,128)S(1)} %get-tuple-element.17) | data formatting | bytes 524288
  53.1 0.6 %copy.13 = f32[72,8]{0,1:T(8,128)} copy(f32[72,8]{0,1:T(8,128)S(1)} %bitcast.3) | data formatting | bytes 4608
  53.7 0.6 %copy.14 = f32[80,8]{0,1:T(8,128)} copy(f32[80,8]{0,1:T(8,128)S(1)} %bitcast.2) | data formatting | bytes 5120

commit v4 on v3

--- a/solution.py
+++ b/solution.py
@@ -13,6 +13,7 @@
 BF16 = jnp.bfloat16
 NN = (((1,), (0,)), ((), ()))
 NT = (((1,), (1,)), ((), ()))
+TN = (((0,), (0,)), ((), ()))
 LANES = 128
 
 
@@ -26,26 +27,48 @@
     return hi, lo
 
 
+def columns(m):
+    n = m.shape[0]
+    return [jnp.broadcast_to(m[:, k : k + 1], (n, LANES)) for k in range(m.shape[1])]
+
+
 def eliminate(gram):
     n = gram.shape[0]
-    row = lax.broadcasted_iota(jnp.int32, (n, n), 0)
-    col = lax.broadcasted_iota(jnp.int32, (n, n), 1)
-    left = gram
-    right = jnp.where(row == col, 1.0, 0.0).astype(F32)
+    row = lax.broadcasted_iota(jnp.int32, (n, LANES), 0)
+    lane = lax.broadcasted_iota(jnp.int32, (n, LANES), 1)
+    left = columns(gram)
+    right = [jnp.where(row == k, 1.0, 0.0).astype(F32) for k in range(n)]
     for j in range(n):
-        factor = jnp.where(row[:, :1] > j, left[:, j : j + 1] / left[j : j + 1, j : j + 1], 0.0)
-        left, right = (left - factor * left[j : j + 1, :], right - factor * right[j : j + 1, :])
-    diag = jnp.sum(jnp.where(row == col, left, 0.0), axis=1, keepdims=True)
+        factor = jnp.where(row > j, left[j] / left[j][j : j + 1], 0.0)
+        left = [c - factor * c[j : j + 1] if k > j else c for k, c in enumerate(left)]
+        right = [c - factor * c[j : j + 1] if k <= j else c for k, c in enumerate(right)]
+    diag = sum(jnp.where(row == k, left[k], 0.0) for k in range(n))
     root = 1.0 / jnp.sqrt(diag)
-    return jnp.where(row <= col, left * root, 0.0), right * root
+    upper = sum(jnp.where((lane == k) & (row <= k), left[k], 0.0) for k in range(n)) * root
+    inverse = sum(jnp.where(lane == k, right[k], 0.0) for k in range(n)) * root
+    return upper[:, 0:n], inverse[:, 0:n]
+
+
+def solve(gram, rhs):
+    n = gram.shape[0]
+    row = lax.broadcasted_iota(jnp.int32, (n, LANES), 0)
+    lane = lax.broadcasted_iota(jnp.int32, (n, LANES), 1)
+    left, right = columns(gram), columns(rhs)
+    for j in range(n):
+        factor = jnp.where(row != j, left[j] / left[j][j : j + 1], 0.0)
+        left = [c - factor * c[j : j + 1] if k > j else c for k, c in enumerate(left)]
+        right = [c - factor * c[j : j + 1] for c in right]
+    diag = sum(jnp.where(row == k, left[k], 0.0) for k in range(n))
+    out = sum(jnp.where(lane == k, right[k], 0.0) for k in range(n)) / diag
+    return out[:, 0:n]
 
 
 def kernel(
     dims,
     b_hbm, p_hbm, codes_hbm,
-    q1_ref, q2_ref, c1_ref, c2_ref,
+    z2, coef_ref, c1_ref, c2_ref,
     xt, wt, codes, rf, up_r, dn_r, pack_l, pack_r, from_l, from_r, wpack_l, wpack_r, wfrom_l, wfrom_r,
-    part, z2, acc, accw, payload, rs_buf, a_buf, b_buf, full,
+    part, acc, accw, payload, rs_buf, a_buf, b_buf, full,
     load_sem, halo_send, halo_recv, red_send, red_recv,
 ):
     nz, nx, ny, rows, nb, np_, scale = dims
@@ -347,65 +370,61 @@
     ga_rows = jnp.concatenate([gb, pltpu.roll(ab_ab, nb, 1)], axis=0)
     w1a, w2a = wa[0:np_], wa[np_:]
     h1 = jnp.where(low, w1a, 0.0)
-    v_a = w1a - small_dot(h1[:, 0:nb], gb, NN)
-    v_w = ww[:, 0:n2] - small_dot(h1, wa, NT)
-    gram = v_w[:, 0:np_] - small_dot(v_a, h1, NT)
+    h1_a = pltpu.roll(h1, nb, 1)
+    n_a = w1a - small_dot(h1[:, 0:nb], gb, NN)
+    n_w = ww[:, 0:n2] - small_dot(h1, wa, NT)
+    an_a = w2a - small_dot(h1_a, ga_rows, NT)
+    an_w = ww[:, n2 : 2 * n2] - small_dot(h1_a, wa, NT)
+    hb = jnp.where(low, an_a, 0.0)
+    gram = n_w[:, 0:np_] - small_dot(n_a, h1, NT)
+    cross = ww[:, np_:n2] - small_dot(w1a, h1_a, NT) - small_dot(h1, hb, NT)
+    y = solve(gram, cross)
     lt1, li1 = eliminate(gram)
-    t_b = -small_dot(li1, h1, NN)
-    t_a = small_dot(li1, v_a, NN)
-    t_w = small_dot(li1, v_w, NN)
-    u_a = pltpu.roll(t_b, nb, 1)
-    gu_a = small_dot(u_a, ga_rows, NT) + small_dot(li1, w2a, NN)
-    gu_w = small_dot(u_a, wa, NT) + small_dot(li1, ww[:, n2 : 2 * n2], NN)
-    h2b = jnp.where(low, gu_a, 0.0)
-    h2q = small_dot(h2b, t_b, NT) + small_dot(gu_w[:, 0:np_], li1, NT)
-    c2a = u_a - h2b - small_dot(h2q, t_b, NN)
-    c2w = -small_dot(h2q, li1, NN)
-    g2a = gu_a - small_dot(h2b[:, 0:nb], gb, NN) - small_dot(h2q, t_a, NN)
-    g2w = gu_w - small_dot(h2b, wa, NT) - small_dot(h2q, t_w, NN)
-    gram = small_dot(c2a, g2a, NT) + small_dot(c2w, g2w[:, 0:np_], NT) + small_dot(li1, g2w[:, np_:], NT)
+    c2a = small_dot(y, h1, TN) - h1_a - hb
+    g2a = an_a - small_dot(hb[:, 0:nb], gb, NN) - small_dot(y, n_a, TN)
+    g2w = an_w - small_dot(hb, wa, NT) - small_dot(y, n_w, TN)
+    gram = small_dot(g2a, c2a, NT) - small_dot(g2w[:, 0:np_], y, NN) + g2w[:, np_:]
     lt2, li2 = eliminate(gram)
-    d_a = small_dot(li2, c2a, NN)
-    d_w = small_dot(li2, c2w, NN)
-    d_v = small_dot(li2, li1, NN)
-    zero = jnp.zeros((np_, np_), F32)
-    coef_a = jnp.concatenate([t_b, d_a], axis=0)
+    h2b = small_dot(li1, hb, NN)
+    h2q = small_dot(small_dot(li1, cross, NT), li1, NT)
+    low2 = small_dot(li1, lt2, NT)
+    coef_a = jnp.concatenate([-small_dot(li1, h1, NN), small_dot(li2, c2a, NN)], axis=0)
     coef_w = jnp.concatenate(
-        [jnp.concatenate([li1, zero], axis=1), jnp.concatenate([d_w, d_v], axis=1)], axis=0
-    )
-    a_hi, a_mid = split_two(coef_a)
-    a_lo = (coef_a - a_hi.astype(F32) - a_mid.astype(F32)).astype(BF16)
-    w_hi, w_mid = split_two(coef_w)
-    w_lo = (coef_w - w_hi.astype(F32) - w_mid.astype(F32)).astype(BF16)
-    a_no, w_no = jnp.zeros_like(a_lo), jnp.zeros_like(w_lo)
-    three = jnp.concatenate(
         [
-            jnp.concatenate([a_hi, a_hi, w_hi, w_hi, w_hi], axis=1),
-            jnp.concatenate([a_mid, a_mid, w_mid, w_mid, w_no], axis=1),
-            jnp.concatenate([a_lo, a_no, w_lo, w_no, w_no], axis=1),
+            jnp.concatenate([li1, jnp.zeros((np_, np_), F32)], axis=1),
+            jnp.concatenate([-small_dot(li2, y, NT), li2], axis=1),
         ],
         axis=0,
     )
-    per = min(8, rows)
-    width = per * LANES
-
-    def last_step(k, _):
-        at = pl.ds(pl.multiple_of(k * width, width), width)
-        o = lax.dot_general(three, z2[:, at], NN, preferred_element_type=F32)
-        out = o[0:n2] + (o[n2 : 2 * n2] + o[2 * n2 :])
-        for i in range(per):
-            q1_ref[:, k * per + i, :] = out[0:np_, i * LANES : (i + 1) * LANES]
-            q2_ref[:, k * per + i, :] = out[np_:, i * LANES : (i + 1) * LANES]
-        return 0
-
-    lax.fori_loop(0, rows // per, last_step, 0)
+    a_hi, a_mid = split_two(coef_a)
+    w_hi, w_mid = split_two(coef_w)
+    coef_ref[...] = jnp.concatenate(
+        [
+            jnp.concatenate([a_hi, a_hi, w_hi, w_hi, w_hi], axis=1),
+            jnp.concatenate([a_mid, a_mid, w_mid, w_mid, jnp.zeros_like(w_mid)], axis=1),
+        ],
+        axis=0,
+    )
 
     def placed(x, first):
         wide = jnp.concatenate([x, jnp.zeros((np_, LANES - np_), F32)], axis=1)
         return pltpu.roll(wide, first, 1)
 
     c1_ref[...] = (h1 + placed(lt1.T, nb))[:, 0:nc]
-    c2_ref[...] = (h2b + placed(h2q, nb) + placed(lt2.T, nc))[:, 0 : nc + np_]
+    c2_ref[...] = (h2b + placed(h2q, nb) + placed(low2, nc))[:, 0 : nc + np_]
+
+
+def product(per, np_, z2, coef_ref, c1_ref, c2_ref, q1_ref, q2_ref, o1_ref, o2_ref):
+    n2 = 2 * np_
+    width = per * LANES
+    at = pl.ds(pl.multiple_of(pl.program_id(0) * width, width), width)
+    o = lax.dot_general(coef_ref[...], z2[:, at], NN, preferred_element_type=F32)
+    out = o[0:n2] + o[n2:]
+    for i in range(per):
+        q1_ref[:, i, :] = out[0:np_, i * LANES : (i + 1) * LANES]
+        q2_ref[:, i, :] = out[np_:, i * LANES : (i + 1) * LANES]
+    o1_ref[...] = c1_ref[...]
+    o2_ref[...] = c2_ref[...]
 
 
 def local(nz, nx, ny, basis, panel, rate_codes):
@@ -421,25 +440,43 @@
         tile(rows + 2, nc), tile(rows + 2, np_), vm((4, rows, LANES), jnp.int32), tile(5, rows + 16),
         vm((8, LANES), jnp.int32), vm((8, LANES), jnp.int32),
         tile(nc), tile(nc), tile(nc), tile(nc), tile(np_), tile(np_), tile(np_), tile(np_),
-        tile(rows, nb), vm((4 * nb + 6 * np_, flat), BF16), vm((4 * nb, 2 * nb), F32), vm((2 * nt, 4 * np_), F32),
+        tile(rows, nb), vm((4 * nb, 2 * nb), F32), vm((2 * nt, 4 * np_), F32),
         tile(nm, 16), tile(nm, 16), tile(ny, 16), tile(nz, 16), tile(nm, 16),
         dma((3,)), dma((14,)), dma((14,)), dma((2 * nm + ny + nz,)), dma((2 * nm + ny + nz,)),
     ]
     vmem = pl.BlockSpec(memory_space=pltpu.VMEM)
+    nz2 = 4 * nb + 6 * np_
+    held = pl.pallas_call(
+        functools.partial(kernel, dims),
+        out_shape=(
+            jax.ShapeDtypeStruct((nz2, flat), BF16),
+            jax.ShapeDtypeStruct((4 * np_, nz2), BF16),
+            jax.ShapeDtypeStruct((np_, nc), F32),
+            jax.ShapeDtypeStruct((np_, nc + np_), F32),
+        ),
+        in_specs=[pl.BlockSpec(memory_space=pltpu.HBM)] * 3,
+        out_specs=(vmem,) * 4,
+        scratch_shapes=scratch,
+        compiler_params=pltpu.CompilerParams(collective_id=0, has_side_effects=True, vmem_limit_bytes=24 << 20),
+        cost_estimate=pl.CostEstimate(flops=10**9, bytes_accessed=4 << 20, transcendentals=0),
+    )(*[pltpu.with_memory_space_constraint(v, pltpu.HBM) for v in (basis, panel, rate_codes)])
+    per = min(16, rows)
+    block = pl.BlockSpec((np_, per, width), lambda k: (0, k, 0))
+    whole = lambda *shape: pl.BlockSpec(shape, lambda k: (0, 0))
     q1, q2, c1, c2 = pl.pallas_call(
-        functools.partial(kernel, dims),
+        functools.partial(product, per, np_),
+        grid=(rows // per,),
         out_shape=(
             jax.ShapeDtypeStruct((np_, rows, width), F32),
             jax.ShapeDtypeStruct((np_, rows, width), F32),
             jax.ShapeDtypeStruct((np_, nc), F32),
             jax.ShapeDtypeStruct((np_, nc + np_), F32),
         ),
-        in_specs=[pl.BlockSpec(memory_space=pltpu.HBM)] * 3,
-        out_specs=(vmem,) * 4,
-        scratch_shapes=scratch,
-        compiler_params=pltpu.CompilerParams(collective_id=0, has_side_effects=True, vmem_limit_bytes=48 << 20),
+        in_specs=[vmem] * 4,
+        out_specs=(block, block, whole(np_, nc), whole(np_, nc + np_)),
+        compiler_params=pltpu.CompilerParams(vmem_limit_bytes=16 << 20),
         cost_estimate=pl.CostEstimate(flops=10**9, bytes_accessed=4 << 20, transcendentals=0),
-    )(*[pltpu.with_memory_space_constraint(v, pltpu.HBM) for v in (basis, panel, rate_codes)])
+    )(*held)
     return (q1, q2, c1.T, c2.T)
 
 

time: 54.4 us -> 50.9 us (0.936)
  local copies, waits for them, and re-layouts: 2.59 us -> 0 us
  Pallas kernels: 51 us -> 50.1 us
    pallas_call x1, Pallas kernels: 51 us -> 47.6 us  [local(): pl.pallas_call(functools.partial(kernel, dims), out_shape=(jax.ShapeDtype...]
    unnamed x4 -> x0, local copies, waits for them, and re-layouts: 2.59 us -> none
    pallas_call x0 -> x1, Pallas kernels: none -> 2.43 us  [local(): pl.pallas_call(functools.partial(product, per, np_), grid=(rows // per,),...]
where the time goes in v4:
time: 50.9 us; the launch traced here: 50.7 us
  Pallas kernels  50.1 us (98%)
  between operations  0.64 us (1%)
    pallas_call x1, Pallas kernels, local(): pl.pallas_call(functools.partial(kernel, dims), out_shape=(jax.ShapeDtype...  47.6 us
    pallas_call x1, Pallas kernels, local(): pl.pallas_call(functools.partial(product, per, np_), grid=(rows // per,),...  2.43 us

profile of v4, /device:TPU:1, one launch (start us, length us, event | category | flops | bytes accessed | tf_op | source)
XLA Modules:
  0.0 50.7 jit_solution(5637740948877590365)
XLA Ops:
  0.6 47.6 %shard_map.66 = (bf16[304,8192]{1,0:T(8,128)(2,1)S(1)}, bf16[32,304]{1,0:T(8,128)(2,1)S(1)}, f32[8,72]{1,0:T(8,128)S(1)}, f32[8,80]{1,0:T(8,128)S(1)}) custom-call(f32[64,64,128]{2,1,0:T(8,128)} %b_hbm.1, f32[8,64,128]{2,1,0:T(8,128)} %p_hbm.1, s32[4,64,128]{2,1,0:T(8,128)} %codes_hbm.1), custom_call_target="tpu_custom_call" | custom-call | flops 1000000000 | bytes 4194304 | tf_op jit(solution)/shard_map/pallas_call | solution.py:449
  48.3 2.4 %shard_map.67 = (f32[8,64,128]{2,1,0:T(8,128)}, f32[8,64,128]{2,1,0:T(8,128)}, f32[8,72]{1,0:T(8,128)}, f32[8,80]{1,0:T(8,128)}) custom-call(bf16[304,8192]{1,0:T(8,128)(2,1)S(1)} %get-tuple-element.12.z2, bf16[32,304]{1,0:T(8,128)(2,1)S(1)} %get-tuple-element.13.coef_ref, f32[8,72]{1,0:T(8,128)S(1)} %get-tuple-element.14.c1_ref, ...), custom_call_target="tpu_custom_call" | custom-call | flops 1000000000 | bytes 4194304 | tf_op jit(solution)/shard_map/pallas_call | solution.py:466

commit v5 on v4

--- a/solution.py
+++ b/solution.py
@@ -227,7 +227,7 @@
 
     has_l, has_r = present(gy > 0), present(gy < ngy - 1)
     for c in small:
-        c.wait()
+        c.wait_recv()
     rf[1, top - 1 : top] = up_r[7:8].astype(F32) * 0.125 * present(gx > 0)
     rf[0, top + rows : top + rows + 1] = dn_r[0:1].astype(F32) * 0.125 * present(gx < ngx - 1)
 
@@ -247,7 +247,7 @@
     ]
 
     for c in big:
-        c.wait()
+        c.wait_recv()
 
     sides_b = both_sides(from_l[0:nb], from_r[0:nb])
 
@@ -271,7 +271,7 @@
     lax.fori_loop(0, end // step, gram_step, 0)
 
     for c in wsend:
-        c.wait()
+        c.wait_recv()
 
     def emit_aw(r, out, c):
         x = jnp.concatenate([wt[r + 1], out], axis=0)
@@ -328,12 +328,26 @@
         c.start()
         return c
 
-    copies = []
-    for d in range(1, nm):
-        copies.append(reduce_copy(d, payload.at[(member + d) % nm], rs_buf.at[member], in_team(d)))
+    def far_first(n, hops):
+        return sorted(range(1, n), key=lambda d: -hops(d))
+
+    def ring(n):
+        return far_first(n, lambda d: min(d, n - d))
+
+    team = far_first(nm, lambda d: min(d, nm - d) + (d == nm // 2 + 1))
+
+    def sent(copies):
+        for c in copies:
+            c.wait_send()
+
+    def arrived(copies):
+        for c in copies:
+            c.wait_recv()
+
+    copies = [reduce_copy(d, payload.at[(member + d) % nm], rs_buf.at[member], in_team(d)) for d in team]
     rs_buf[member, 0:per_all] = payload[member, 0:per_all]
-    for c in copies:
-        c.wait()
+    sent(small + big + wsend)
+    arrived(copies)
 
     def ordered_sum(buf, n):
         total = buf[0, 0:per_all]
@@ -343,20 +357,22 @@
 
     one = yy * (1 - core) + zz * core
     two = zz * (1 - core) + yy * core
+    last = copies
     a_buf[one, 0:per_all] = ordered_sum(rs_buf, nm)
-    copies = [reduce_copy(nm + d, a_buf.at[one], a_buf.at[one], in_first(d)) for d in range(1, ny)]
-    for c in copies:
-        c.wait()
+    copies = [reduce_copy(nm + d, a_buf.at[one], a_buf.at[one], in_first(d)) for d in ring(ny)]
+    sent(last)
+    arrived(copies)
+    last = copies
     b_buf[two, 0:per_all] = ordered_sum(a_buf, ny)
-    copies = [reduce_copy(nm + ny + d, b_buf.at[two], b_buf.at[two], in_second(d)) for d in range(1, nz)]
-    for c in copies:
-        c.wait()
+    copies = [reduce_copy(nm + ny + d, b_buf.at[two], b_buf.at[two], in_second(d)) for d in ring(nz)]
+    sent(last)
+    arrived(copies)
+    last = copies
     full[member, 0:per_all] = ordered_sum(b_buf, nz)
-    copies = [
-        reduce_copy(nm + ny + nz + d, full.at[member], full.at[member], in_team(d)) for d in range(1, nm)
-    ]
-    for c in copies:
-        c.wait()
+    copies = [reduce_copy(nm + ny + nz + d, full.at[member], full.at[member], in_team(d)) for d in team]
+    sent(last)
+    arrived(copies)
+    last = copies
 
     main = jnp.concatenate([full[m, 0:per_main] for m in range(nm)], axis=0) * scale
     extra = jnp.concatenate([full[m, per_main:per_all] for m in range(nm)], axis=0) * scale
@@ -410,6 +426,7 @@
         wide = jnp.concatenate([x, jnp.zeros((np_, LANES - np_), F32)], axis=1)
         return pltpu.roll(wide, first, 1)
 
+    sent(last)
     c1_ref[...] = (h1 + placed(lt1.T, nb))[:, 0:nc]
     c2_ref[...] = (h2b + placed(h2q, nb) + placed(low2, nc))[:, 0 : nc + np_]
 
@@ -460,7 +477,7 @@
         compiler_params=pltpu.CompilerParams(collective_id=0, has_side_effects=True, vmem_limit_bytes=24 << 20),
         cost_estimate=pl.CostEstimate(flops=10**9, bytes_accessed=4 << 20, transcendentals=0),
     )(*[pltpu.with_memory_space_constraint(v, pltpu.HBM) for v in (basis, panel, rate_codes)])
-    per = min(16, rows)
+    per = min(32, rows)
     block = pl.BlockSpec((np_, per, width), lambda k: (0, k, 0))
     whole = lambda *shape: pl.BlockSpec(shape, lambda k: (0, 0))
     q1, q2, c1, c2 = pl.pallas_call(

time: 50.9 us -> 49.6 us (0.974)
  Pallas kernels: 50.1 us -> 48.8 us
    pallas_call x1, Pallas kernels: 47.6 us -> 46.8 us  [local(): pl.pallas_call(functools.partial(kernel, dims), out_shape=(jax.ShapeDtype...]
where the time goes in v5:
time: 49.6 us; the launch traced here: 49.4 us
  Pallas kernels  48.8 us (98%)
  between operations  0.64 us (1%)
    pallas_call x1, Pallas kernels, local(): pl.pallas_call(functools.partial(kernel, dims), out_shape=(jax.ShapeDtype...  46.8 us
    pallas_call x1, Pallas kernels, local(): pl.pallas_call(functools.partial(product, per, np_), grid=(rows // per,),...  1.95 us

profile of v5, /device:TPU:1, one launch (start us, length us, event | category | flops | bytes accessed | tf_op | source)
XLA Modules:
  0.0 49.4 jit_solution(11763834065986834067)
XLA Ops:
  0.6 46.8 %shard_map.66 = (bf16[304,8192]{1,0:T(8,128)(2,1)S(1)}, bf16[32,304]{1,0:T(8,128)(2,1)S(1)}, f32[8,72]{1,0:T(8,128)S(1)}, f32[8,80]{1,0:T(8,128)S(1)}) custom-call(f32[64,64,128]{2,1,0:T(8,128)} %b_hbm.1, f32[8,64,128]{2,1,0:T(8,128)} %p_hbm.1, s32[4,64,128]{2,1,0:T(8,128)} %codes_hbm.1), custom_call_target="tpu_custom_call" | custom-call | flops 1000000000 | bytes 4194304 | tf_op jit(solution)/shard_map/pallas_call | solution.py:466
  47.5 1.9 %shard_map.67 = (f32[8,64,128]{2,1,0:T(8,128)}, f32[8,64,128]{2,1,0:T(8,128)}, f32[8,72]{1,0:T(8,128)}, f32[8,80]{1,0:T(8,128)}) custom-call(bf16[304,8192]{1,0:T(8,128)(2,1)S(1)} %get-tuple-element.12.z2, bf16[32,304]{1,0:T(8,128)(2,1)S(1)} %get-tuple-element.13.coef_ref, f32[8,72]{1,0:T(8,128)S(1)} %get-tuple-element.14.c1_ref, ...), custom_call_target="tpu_custom_call" | custom-call | flops 1000000000 | bytes 4194304 | tf_op jit(solution)/shard_map/pallas_call | solution.py:483

commit v6 on v5

--- a/solution.py
+++ b/solution.py
@@ -131,16 +131,15 @@
         a, b = accs
         return (jnp.where(lane == 2 * r, y, a), jnp.where(lane == (2 * r + LANES - 1) % LANES, y, b))
 
-    def pack(at, n):
-        per = 8
-
+    def pack(at, n, per):
         def body(k, accs):
             for i in range(per):
                 accs = pack_step(xt[k * per + i + 1, at], k * per + i, accs)
             return accs
 
         zero = jnp.zeros((n, LANES), F32)
-        a, b = lax.fori_loop(0, rows // per, body, (zero, zero))
+        carry = (zero, zero)
+        a, b = body(0, carry) if per == rows else lax.fori_loop(0, rows // per, body, carry)
         pack_l[at] = a
         pack_r[at] = b
 
@@ -149,7 +148,7 @@
     rf[0:4, top : top + rows] = values
     rf[4, top : top + rows] = values[0] + values[1] + values[2] + values[3]
     pltpu.make_async_copy(p_hbm, xt.at[inner, nb:nc], load_sem.at[1]).wait()
-    pack(slice(nb, nc), np_)
+    pack(slice(nb, nc), np_, rows)
 
     pl.semaphore_wait(barrier, len(peers))
 
@@ -174,7 +173,7 @@
         halo(6, xt.at[rows, 0:nb], xt.at[0, 0:nb], below),
         halo(7, xt.at[1, 0:nb], xt.at[rows + 1, 0:nb], above),
     ]
-    pack(slice(0, nb), nb)
+    pack(slice(0, nb), nb, 16)
     big += [
         halo(8, pack_r.at[0:nb], from_l.at[0:nb], right),
         halo(9, pack_l.at[0:nb], from_r.at[0:nb], left),
@@ -200,14 +199,14 @@
         return rate(1, r - 1) * xu + rate(0, r + 1) * xd + jnp.where((lane == 0) | (lane == LANES - 1), side, 0.0)
 
     def own_step(k, _):
-        for i in range(4):
-            r = 4 * k + i
+        for i in range(8):
+            r = 8 * k + i
             x = xt[r + 1, 0:nb]
             put(0, r, x)
             part[r] = own(r, x)
         return 0
 
-    lax.fori_loop(0, rows // 4, own_step, 0)
+    lax.fori_loop(0, rows // 8, own_step, 0)
 
     def sweep(x_at, sides, emit, carry, per):
         def body(k, c):
@@ -217,7 +216,7 @@
                 c = emit(r, out, c)
             return c
 
-        return lax.fori_loop(0, rows // per, body, carry)
+        return body(0, carry) if per == rows else lax.fori_loop(0, rows // per, body, carry)
 
     def both_sides(fl, fr):
         return jnp.where(lane % 2 == 0, fr * has_r, pltpu.roll(fl, 2, 1) * has_l)
@@ -236,7 +235,7 @@
         return pack_step(out, r, accs)
 
     zp = jnp.zeros((np_, LANES), F32)
-    a, b = sweep(lambda r: xt[r + 1, nb:nc], both_sides(from_l[nb:nc], from_r[nb:nc]), emit_w, (zp, zp), 16)
+    a, b = sweep(lambda r: xt[r + 1, nb:nc], both_sides(from_l[nb:nc], from_r[nb:nc]), emit_w, (zp, zp), rows)
     wpack_l[...] = a
     wpack_r[...] = b
     wsend = [
@@ -252,12 +251,12 @@
     sides_b = both_sides(from_l[0:nb], from_r[0:nb])
 
     def other_step(k, _):
-        for i in range(4):
-            r = 4 * k + i
+        for i in range(8):
+            r = 8 * k + i
             put(nb, r, part[r] + other(r, xt[r, 0:nb], xt[r + 2, 0:nb], sides_b))
         return 0
 
-    lax.fori_loop(0, rows // 4, other_step, 0)
+    lax.fori_loop(0, rows // 8, other_step, 0)
 
     end = rows * LANES
     step = min(2048, end)
@@ -281,18 +280,18 @@
         z2[2 * na + 2 * n2 :, at_row(r)] = (x - hi.astype(F32) - lo.astype(F32)).astype(BF16)
         return c
 
-    sweep(lambda r: wt[r + 1], both_sides(wfrom_l[...], wfrom_r[...]), emit_aw, 0, 16)
-
-    accw[...] = jnp.zeros_like(accw)
-
-    def gram_w_step(k, _):
-        at = pl.ds(pl.multiple_of(k * step, step), step)
-        accw[...] += lax.dot_general(
+    sides_w = both_sides(wfrom_l[...], wfrom_r[...])
+    total_w = None
+    span = 16
+    for k in range(rows // span):
+        for r in range(k * span, (k + 1) * span):
+            emit_aw(r, own(r, wt[r + 1]) + other(r, wt[r], wt[r + 2], sides_w), 0)
+        at = slice(k * span * LANES, (k + 1) * span * LANES)
+        term = lax.dot_general(
             z2[0 : 2 * na + 2 * n2, at], z2[2 * na : 2 * na + 2 * n2, at], NT, preferred_element_type=F32
         )
-        return 0
-
-    lax.fori_loop(0, end // step, gram_w_step, 0)
+        total_w = term if total_w is None else total_w + term
+    accw[...] = total_w
     aa = acc[0:na] * 0.5 + acc[na : 2 * na]
     aa = aa + aa.T
     by_w = accw[...]

time: 49.6 us -> 47.9 us (0.966)
  Pallas kernels: 48.8 us -> 47.1 us
    pallas_call x1, Pallas kernels: 46.8 us -> 45.1 us  [local(): pl.pallas_call(functools.partial(kernel, dims), out_shape=(jax.ShapeDtype...]
where the time goes in v6:
time: 47.9 us; the launch traced here: 47.7 us
  Pallas kernels  47.1 us (98%)
  between operations  0.64 us (1%)
    pallas_call x1, Pallas kernels, local(): pl.pallas_call(functools.partial(kernel, dims), out_shape=(jax.ShapeDtype...  45.1 us
    pallas_call x1, Pallas kernels, local(): pl.pallas_call(functools.partial(product, per, np_), grid=(rows // per,),...  1.95 us

profile of v6, /device:TPU:1, one launch (start us, length us, event | category | flops | bytes accessed | tf_op | source)
XLA Modules:
  0.0 47.7 jit_solution(5518677710881592234)
XLA Ops:
  0.6 45.1 %shard_map.66 = (bf16[304,8192]{1,0:T(8,128)(2,1)S(1)}, bf16[32,304]{1,0:T(8,128)(2,1)S(1)}, f32[8,72]{1,0:T(8,128)S(1)}, f32[8,80]{1,0:T(8,128)S(1)}) custom-call(f32[64,64,128]{2,1,0:T(8,128)} %b_hbm.1, f32[8,64,128]{2,1,0:T(8,128)} %p_hbm.1, s32[4,64,128]{2,1,0:T(8,128)} %codes_hbm.1), custom_call_target="tpu_custom_call" | custom-call | flops 1000000000 | bytes 4194304 | tf_op jit(solution)/shard_map/pallas_call | solution.py:465
  45.8 2.0 %shard_map.67 = (f32[8,64,128]{2,1,0:T(8,128)}, f32[8,64,128]{2,1,0:T(8,128)}, f32[8,72]{1,0:T(8,128)}, f32[8,80]{1,0:T(8,128)}) custom-call(bf16[304,8192]{1,0:T(8,128)(2,1)S(1)} %get-tuple-element.12.z2, bf16[32,304]{1,0:T(8,128)(2,1)S(1)} %get-tuple-element.13.coef_ref, f32[8,72]{1,0:T(8,128)S(1)} %get-tuple-element.14.c1_ref, ...), custom_call_target="tpu_custom_call" | custom-call | flops 1000000000 | bytes 4194304 | tf_op jit(solution)/shard_map/pallas_call | solution.py:482

commit v7 on v6

--- a/solution.py
+++ b/solution.py
@@ -199,14 +199,14 @@
         return rate(1, r - 1) * xu + rate(0, r + 1) * xd + jnp.where((lane == 0) | (lane == LANES - 1), side, 0.0)
 
     def own_step(k, _):
-        for i in range(8):
-            r = 8 * k + i
+        for i in range(16):
+            r = 16 * k + i
             x = xt[r + 1, 0:nb]
             put(0, r, x)
             part[r] = own(r, x)
         return 0
 
-    lax.fori_loop(0, rows // 8, own_step, 0)
+    lax.fori_loop(0, rows // 16, own_step, 0)
 
     def sweep(x_at, sides, emit, carry, per):
         def body(k, c):
@@ -251,12 +251,12 @@
     sides_b = both_sides(from_l[0:nb], from_r[0:nb])
 
     def other_step(k, _):
-        for i in range(8):
-            r = 8 * k + i
+        for i in range(16):
+            r = 16 * k + i
             put(nb, r, part[r] + other(r, xt[r, 0:nb], xt[r + 2, 0:nb], sides_b))
         return 0
 
-    lax.fori_loop(0, rows // 8, other_step, 0)
+    lax.fori_loop(0, rows // 16, other_step, 0)
 
     end = rows * LANES
     step = min(2048, end)

time: 47.9 us -> 47.8 us (level)
  no operation moved by 1% of the time
where the time goes in v7:
time: 47.8 us; the launch traced here: 47.7 us
  Pallas kernels  47 us (98%)
  between operations  0.64 us (1%)
    pallas_call x1, Pallas kernels, local(): pl.pallas_call(functools.partial(kernel, dims), out_shape=(jax.ShapeDtype...  45.1 us
    pallas_call x1, Pallas kernels, local(): pl.pallas_call(functools.partial(product, per, np_), grid=(rows // per,),...  1.95 us

profile of v7, /device:TPU:1, one launch (start us, length us, event | category | flops | bytes accessed | tf_op | source)
XLA Modules:
  0.0 47.7 jit_solution(7320137757045554316)
XLA Ops:
  0.6 45.1 %shard_map.66 = (bf16[304,8192]{1,0:T(8,128)(2,1)S(1)}, bf16[32,304]{1,0:T(8,128)(2,1)S(1)}, f32[8,72]{1,0:T(8,128)S(1)}, f32[8,80]{1,0:T(8,128)S(1)}) custom-call(f32[64,64,128]{2,1,0:T(8,128)} %b_hbm.1, f32[8,64,128]{2,1,0:T(8,128)} %p_hbm.1, s32[4,64,128]{2,1,0:T(8,128)} %codes_hbm.1), custom_call_target="tpu_custom_call" | custom-call | flops 1000000000 | bytes 4194304 | tf_op jit(solution)/shard_map/pallas_call | solution.py:465
  45.7 2.0 %shard_map.67 = (f32[8,64,128]{2,1,0:T(8,128)}, f32[8,64,128]{2,1,0:T(8,128)}, f32[8,72]{1,0:T(8,128)}, f32[8,80]{1,0:T(8,128)}) custom-call(bf16[304,8192]{1,0:T(8,128)(2,1)S(1)} %get-tuple-element.12.z2, bf16[32,304]{1,0:T(8,128)(2,1)S(1)} %get-tuple-element.13.coef_ref, f32[8,72]{1,0:T(8,128)S(1)} %get-tuple-element.14.c1_ref, ...), custom_call_target="tpu_custom_call" | custom-call | flops 1000000000 | bytes 4194304 | tf_op jit(solution)/shard_map/pallas_call | solution.py:482
